TPU v7x, 8 devices: a whole 2x2x1 slice. The times are simulated.
8 devices in a mesh: dp: 2 (over z, y), ep: 4 (over x, core).
Axes of the slice: x: 2, y: 2, z: 1, core: 2. Of those that a mesh axis runs over, the one named last changes fastest.
Arguments:
- w_gate: bfloat16 [1, 8, 4096, 1536], P(None, 'ep')
- w_up: bfloat16 [1, 8, 4096, 1536], P(None, 'ep')
- w_down: bfloat16 [1, 8, 1536, 4096], P(None, 'ep')
- place: int32 [1, 32], replicated
Outputs:
- output 1: bfloat16 [1, 32, 4096, 3072], P(None, ('dp', 'ep'))
- output 2: bfloat16 [1, 32, 1536, 4096], P(None, ('dp', 'ep'))
All inputs are finite; a program needn't handle non-finite values.
Results may differ from a plain program's by a relative error of at most 0.001.
Values are sent between devices in bfloat16 or wider.
A program may use at most 1 GiB of HBM per device.

v0:
```python
import jax
import jax.numpy as jnp
import numpy as np
from jax import lax
from jax.sharding import PartitionSpec as P


def _routes(dp, ep, slots):
    n_dev = dp * ep
    out = []
    for j in range(slots):
        pairs, send_to, local = [], list(range(n_dev)), [False] * n_dev
        for a in range(dp):
            for g in range(ep):
                h = (2 * a - g) % ep if j < ((a + 1) * slots) // dp else (g + j + 1) % ep
                n = a * ep + g
                if h == g:
                    local[n] = True
                    continue
                src = ((a + j) % dp) * ep + h
                pairs.append((src, n))
                send_to[src] = n
        out.append((pairs, send_to, local))
    return out


def solution(mesh):
    dp = mesh.shape["dp"]
    ep = mesh.shape["ep"]
    n_dev = dp * ep

    def body(w_gate, w_up, w_down, place):
        g = lax.axis_index("ep")
        me = lax.axis_index("dp") * ep + g
        n_exp = w_gate.shape[1]
        slots = place.shape[1] // n_dev
        routes = _routes(dp, ep, slots)
        take = jax.vmap(lambda w, i: w[i])
        own = jnp.clip(lax.dynamic_slice_in_dim(place, me * slots, slots, axis=1) - g * n_exp, 0, n_exp - 1)
        own13 = jnp.concatenate([take(w_gate, own), take(w_up, own)], axis=-1)
        own2 = take(w_down, own)
        got13, got2 = [], []
        for j, (pairs, send_to, _) in enumerate(routes):
            dst = jnp.asarray(np.array(send_to, np.int32))[me]
            idx = jnp.clip(place[:, dst * slots + j] - g * n_exp, 0, n_exp - 1)
            b13 = jnp.concatenate([take(w_gate, idx), take(w_up, idx)], axis=-1)
            b2 = take(w_down, idx)
            if pairs:
                b13 = lax.ppermute(b13, ("dp", "ep"), pairs)
                b2 = lax.ppermute(b2, ("dp", "ep"), pairs)
            got13.append(b13)
            got2.append(b2)
        local = jnp.asarray(np.array([r[2] for r in routes], bool).T)[me][None, :, None, None]
        w13 = jnp.where(local, own13, jnp.stack(got13, axis=1))
        w2 = jnp.where(local, own2, jnp.stack(got2, axis=1))
        return w13, w2

    spec_in = P(None, "ep", None, None)
    spec_out = P(None, ("dp", "ep"), None, None)
    return jax.shard_map(body, mesh=mesh,
                         in_specs=(spec_in, spec_in, spec_in, P(None, None)),
                         out_specs=(spec_out, spec_out), check_vma=False)
```

profile of v0, /device:TPU:0, one launch (start us, length us, event | category | flops | bytes accessed | tf_op | source)
XLA Modules:
  0.0 1819.9 jit_solution(14990359429299253693)
XLA Ops:
  12.2 67.6 %dynamic-slice_bitcast_fusion.10 = (bf16[1,4096,1536]{2,1,0:T(8,128)(2,1)}, bf16[1,4096,1536]{2,1,0:T(8,128)(2,1)}, bf16[1,4096,1536]{2,1,0:T(8,128)(2,1)}, bf16...) fusion(bf16[1,2,4096,1536]{3,2,1,0:T(8,128)(2,1)} %param.10, ...), kind=kLoop, calls=%fused_computation.37 | loop fusion | bytes 201326608 | tf_op jit(solution)/shard_map/vmap()/squeeze | solution.py:38
  79.8 20.8 %pad_maximum_fusion = bf16[1,4096,3072]{2,1,0:T(8,128)(2,1)} fusion(bf16[1,4096,1536]{2,1,0:T(8,128)(2,1)} %get-tuple-element.148, bf16[1,4096,1536]{2,1,0:T(8,128)(2,1)} %get-tuple-element.171), kind=kLoop, calls=%fused_computation.23 | loop fusion | flops 50331648 | bytes 50331648 | tf_op jit(solution)/shard_map/concatenate | solution.py:46
  100.6 9.0 collective-permute-start
  109.6 33.9 %dynamic-slice_bitcast_fusion.3 = (bf16[1,1536,4096]{2,1,0:T(8,128)(2,1)}, bf16[1,1536,4096]{2,1,0:T(8,128)(2,1)}, bf16[1,1536,4096]{2,1,0:T(8,128)(2,1)}, bf16[1,1536,4096]{2,1,0:T(8,128)(2,1)}) fusion(bf16[1,2,1536,4096]{3,2,1,0:T(8,128)(2,1)} %param.11, s32[]{:T(128)} %bitcast.21, s32[]{:T(128)} %bitcast.35, s32[]{:T(128)} %bitcast.28, s32[]{:T(128)} %bitcast.42), kind=kLoop, calls=%fused_computation.30 | loop fusion | bytes 100663312 | tf_op jit(solution)/shard_map/vmap()/squeeze | solution.py:38
  162.1 17.0 fusion.5
  179.1 17.6 fusion.4
  216.9 7.1 bitcast_dynamic-update-slice_fusion.5
  256.9 7.1 bitcast_dynamic-update-slice_fusion.4
  264.0 7.3 bitcast_dynamic-update-slice_fusion.3
  271.3 7.3 bitcast_dynamic-update-slice_fusion.2
  282.5 16.9 fusion.6
  299.4 20.9 %pad_maximum_fusion.1 = bf16[1,4096,3072]{2,1,0:T(8,128)(2,1)} fusion(bf16[1,4096,1536]{2,1,0:T(8,128)(2,1)} %get-tuple-element.150, bf16[1,4096,1536]{2,1,0:T(8,128)(2,1)} %get-tuple-element.169), kind=kLoop, calls=%fused_computation.24 | loop fusion | flops 50331648 | bytes 50331648 | tf_op jit(solution)/shard_map/concatenate | solution.py:46
  320.3 20.9 %pad_maximum_fusion.2 = bf16[1,4096,3072]{2,1,0:T(8,128)(2,1)} fusion(bf16[1,4096,1536]{2,1,0:T(8,128)(2,1)} %get-tuple-element.149, bf16[1,4096,1536]{2,1,0:T(8,128)(2,1)} %get-tuple-element.170), kind=kLoop, calls=%fused_computation.25 | loop fusion | flops 50331648 | bytes 50331648 | tf_op jit(solution)/shard_map/concatenate | solution.py:46
  341.2 20.9 %pad_maximum_fusion.3 = bf16[1,4096,3072]{2,1,0:T(8,128)(2,1)} fusion(bf16[1,4096,1536]{2,1,0:T(8,128)(2,1)} %get-tuple-element.151, bf16[1,4096,1536]{2,1,0:T(8,128)(2,1)} %get-tuple-element.168), kind=kLoop, calls=%fused_computation.26 | loop fusion | flops 50331648 | bytes 50331648 | tf_op jit(solution)/shard_map/concatenate | solution.py:46
  362.0 7.1 bitcast_dynamic-update-slice_fusion
  450.4 209.5 %collective-permute-start.1 = (bf16[1,4096,3072]{2,1,0:T(8,128)(2,1)}, bf16[1,4096,3072]{2,1,0:T(8,128)(2,1)}, u32[]{:S(2)}, u32[]{:S(2)}) collective-permute-start(bf16[1,4096,3072]{2,1,0:T(8,128)(2,1)} %pad_maximum_fusion.1), channel_id=1, source_target_pairs={{7,1},{5,3},{2,4},{0,6}} | collective-permute-start | bytes 75497480 | tf_op jit(solution)/shard_map/ppermute | solution.py:49
  659.8 213.9 %collective-permute-start.2 = (bf16[1,4096,3072]{2,1,0:T(8,128)(2,1)}, bf16[1,4096,3072]{2,1,0:T(8,128)(2,1)}, u32[]{:S(2)}, u32[]{:S(2)}) collective-permute-start(bf16[1,4096,3072]{2,1,0:T(8,128)(2,1)} %pad_maximum_fusion.2), channel_id=1, source_target_pairs={{3,0},{0,1},{1,2},{2,3},{6,4},{4,6}} | collective-permute-start | bytes 75497480 | tf_op jit(solution)/shard_map/ppermute | solution.py:49
  873.8 264.1 %collective-permute-done.6 = bf16[1,1536,4096]{2,1,0:T(8,128)(2,1)} collective-permute-done((bf16[1,1536,4096]{2,1,0:T(8,128)(2,1)}, bf16[1,1536,4096]{2,1,0:T(8,128)(2,1)}, u32[]{:S(2)}, u32[]{:S(2)}) %collective-permute-start.6) | collective-permute-done | bytes 12582944 | tf_op jit(solution)/shard_map/ppermute | solution.py:50
  1137.9 9.6 collective-permute-start.3
  1149.3 7.1 bitcast_dynamic-update-slice_fusion.11
  1219.4 48.0 %maximum_select_fusion.1 = bf16[1,4,1536,4096]{3,2,1,0:T(8,128)(2,1)} fusion(bf16[1,4,1536,4096]{3,2,1,0:T(8,128)(2,1)} %bitcast_dynamic-update-slice_fusion.18, bf16[1,1,1536,4096]{3,2,1,0:T(8,128)(2,1)} %bitcast.60, bf16[1,1,1536,4096]{3,2,1,0:T(8,128)(2,1)} %bitcast.58, bf16[1,1,1536,4096]{3,2,1,0:T(8,128)(2,1)} %bitcast.56, ...), kind=kLoop, calls=%fused_computation.22 | loop fusion | flops 100663296 | bytes 150994944 | tf_op jit(solution)/shard_map/jit(_where)/select_n | solution.py:55
  1267.5 409.7 %collective-permute-done.2 = bf16[1,4096,3072]{2,1,0:T(8,128)(2,1)} collective-permute-done((bf16[1,4096,3072]{2,1,0:T(8,128)(2,1)}, bf16[1,4096,3072]{2,1,0:T(8,128)(2,1)}, u32[]{:S(2)}, u32[]{:S(2)}) %collective-permute-start.2) | collective-permute-done | bytes 25165856 | tf_op jit(solution)/shard_map/ppermute | solution.py:49
  1677.2 46.9 %collective-permute-done.3 = bf16[1,4096,3072]{2,1,0:T(8,128)(2,1)} collective-permute-done((bf16[1,4096,3072]{2,1,0:T(8,128)(2,1)}, bf16[1,4096,3072]{2,1,0:T(8,128)(2,1)}, u32[]{:S(2)}, u32[]{:S(2)}) %collective-permute-start.3) | collective-permute-done | bytes 25165856 | tf_op jit(solution)/shard_map/ppermute | solution.py:49
  1724.1 95.6 %maximum_select_fusion = bf16[1,4,4096,3072]{3,2,1,0:T(8,128)(2,1)} fusion(bf16[1,4,4096,1536]{3,2,1,0:T(8,128)(2,1)} %get-tuple-element.172, bf16[1,4,4096,1536]{3,2,1,0:T(8,128)(2,1)} %get-tuple-element.173, bf16[1,1,4096,3072]{3,2,1,0:T(8,128)(2,1)} %bitcast.45, bf16[1,1,4096,3072]{3,2,1,0:T(8,128)(2,1)} %bitcast.38, ...), kind=kLoop, calls=%fused_computation.21 | loop fusion | flops 654311424 | bytes 301989888 | tf_op jit(solution)/shard_map/jit(_where)/select_n | solution.py:54
  (86 shorter events, 228.0 us)
Async XLA Ops:
  100.6 1166.8 %collective-permute-start = (bf16[1,4096,3072]{2,1,0:T(8,128)(2,1)}, bf16[1,4096,3072]{2,1,0:T(8,128)(2,1)}, u32[]{:S(2)}, u32[]{:S(2)}) collective-permute-start(bf16[1,4096,3072]{2,1,0:T(8,128)(2,1)} %pad_maximum_fusion), channel_id=1, source_target_pairs={{3,1},{1,3},{6,4},{4,6}} | collective-permute-start | bytes 75497480 | tf_op jit(solution)/shard_map/ppermute | solution.py:49
  143.5 306.9 %collective-permute-start.4 = (bf16[1,1536,4096]{2,1,0:T(8,128)(2,1)}, bf16[1,1536,4096]{2,1,0:T(8,128)(2,1)}, u32[]{:S(2)}, u32[]{:S(2)}) collective-permute-start(bf16[1,1536,4096]{2,1,0:T(8,128)(2,1)} %get-tuple-element.134), channel_id=1, source_target_pairs={{3,1},{1,3},{6,4},{4,6}} | collective-permute-start | bytes 37748744 | tf_op jit(solution)/shard_map/ppermute | solution.py:50
  148.6 511.2 %collective-permute-start.5 = (bf16[1,1536,4096]{2,1,0:T(8,128)(2,1)}, bf16[1,1536,4096]{2,1,0:T(8,128)(2,1)}, u32[]{:S(2)}, u32[]{:S(2)}) collective-permute-start(bf16[1,1536,4096]{2,1,0:T(8,128)(2,1)} %get-tuple-element.136), channel_id=1, source_target_pairs={{7,1},{5,3},{2,4},{0,6}} | collective-permute-start | bytes 37748744 | tf_op jit(solution)/shard_map/ppermute | solution.py:50
  154.4 983.5 %collective-permute-start.6 = (bf16[1,1536,4096]{2,1,0:T(8,128)(2,1)}, bf16[1,1536,4096]{2,1,0:T(8,128)(2,1)}, u32[]{:S(2)}, u32[]{:S(2)}) collective-permute-start(bf16[1,1536,4096]{2,1,0:T(8,128)(2,1)} %get-tuple-element.135), channel_id=1, source_target_pairs={{3,0},{0,1},{1,2},{2,3},{6,4},{4,6}} | collective-permute-start | bytes 37748744 | tf_op jit(solution)/shard_map/ppermute | solution.py:50
  156.3 1063.1 %collective-permute-start.7 = (bf16[1,1536,4096]{2,1,0:T(8,128)(2,1)}, bf16[1,1536,4096]{2,1,0:T(8,128)(2,1)}, u32[]{:S(2)}, u32[]{:S(2)}) collective-permute-start(bf16[1,1536,4096]{2,1,0:T(8,128)(2,1)} %get-tuple-element.137), channel_id=1, source_target_pairs={{2,4},{0,6}} | collective-permute-start | bytes 37748744 | tf_op jit(solution)/shard_map/ppermute | solution.py:50
  179.1 17.6 copy-start.2
  264.0 14.6 slice-start.8
  271.3 7.3 slice-start.9
  430.1 13.1 slice-start
  436.6 9.0 slice-start.1
  443.2 7.1 copy-start.3
  450.3 706.1 %slice-start.6 = ((s8[7864320]{0:T(1024)(128)(4,1)}), s8[4194304]{0:T(1024)(128)(4,1)S(1)}, s32[]{:S(2)}) async-start(s8[7864320]{0:T(1024)(128)(4,1)} %bitcast.102), calls=%async_computation.6 | async-start | bytes 8388608
  450.4 817.1 %collective-permute-start.1 = (bf16[1,4096,3072]{2,1,0:T(8,128)(2,1)}, bf16[1,4096,3072]{2,1,0:T(8,128)(2,1)}, u32[]{:S(2)}, u32[]{:S(2)}) collective-permute-start(bf16[1,4096,3072]{2,1,0:T(8,128)(2,1)} %pad_maximum_fusion.1), channel_id=1, source_target_pairs={{7,1},{5,3},{2,4},{0,6}} | collective-permute-start | bytes 75497480 | tf_op jit(solution)/shard_map/ppermute | solution.py:49
  659.8 1017.4 %collective-permute-start.2 = (bf16[1,4096,3072]{2,1,0:T(8,128)(2,1)}, bf16[1,4096,3072]{2,1,0:T(8,128)(2,1)}, u32[]{:S(2)}, u32[]{:S(2)}) collective-permute-start(bf16[1,4096,3072]{2,1,0:T(8,128)(2,1)} %pad_maximum_fusion.2), channel_id=1, source_target_pairs={{3,0},{0,1},{1,2},{2,3},{6,4},{4,6}} | collective-permute-start | bytes 75497480 | tf_op jit(solution)/shard_map/ppermute | solution.py:49
  1137.9 586.2 %collective-permute-start.3 = (bf16[1,4096,3072]{2,1,0:T(8,128)(2,1)}, bf16[1,4096,3072]{2,1,0:T(8,128)(2,1)}, u32[]{:S(2)}, u32[]{:S(2)}) collective-permute-start(bf16[1,4096,3072]{2,1,0:T(8,128)(2,1)} %pad_maximum_fusion.3), channel_id=1, source_target_pairs={{2,4},{0,6}} | collective-permute-start | bytes 75497480 | tf_op jit(solution)/shard_map/ppermute | solution.py:49
  1149.3 7.1 slice-start.7
  1160.1 14.1 slice-start.4
  1167.1 7.0 slice-start.5
  1191.6 13.9 slice-start.2
  1198.6 7.0 slice-start.3
  1209.3 7.0 copy-start
  1209.3 7.0 copy-start.1
where the time goes:
time: 1820 us
  waiting for transfers between devices  721 us (40%)
  starting transfers between devices  461 us (25%)
  local copies, waits for them, and re-layouts  405 us (22%)
  other arithmetic  227 us (12%)
    ppermute x4, waiting for transfers between devices, body(): b13 = lax.ppermute(b13, ('dp', 'ep'), pairs)  457 us
    ppermute x4, starting transfers between devices, body(): b13 = lax.ppermute(b13, ('dp', 'ep'), pairs)  442 us
    ppermute x4, waiting for transfers between devices, body(): b2 = lax.ppermute(b2, ('dp', 'ep'), pairs)  264 us
    gather x30, local copies, waits for them, and re-layouts, body(): take = jax.vmap(lambda w, i: w[i])  179 us
    unnamed x44, local copies, waits for them, and re-layouts  119 us
    squeeze x2, local copies, waits for them, and re-layouts, body(): take = jax.vmap(lambda w, i: w[i])  101 us
    select_n x1, other arithmetic, body(): w13 = jnp.where(local, own13, jnp.stack(got13, axis=1))  95.6 us
    concatenate x4, other arithmetic, body(): b13 = jnp.concatenate([take(w_gate, idx), take(w_up, idx)], axis=-1)  83.5 us
  transfers between devices with their start and end apart: 8, of which 3 were waited for; matrix products, arithmetic and copies ran while one was open for 24% of the time, Pallas kernels for 0%

commit v1 on v0

v1 whole, which is shorter than its diff:
```python
import functools

import jax
import jax.numpy as jnp
from jax import lax
from jax.experimental import pallas as pl
from jax.experimental.pallas import tpu as pltpu
from jax.sharding import PartitionSpec as P


TILE = 256
NBUF = 8
LAG = 3
DOWN = (768, 384, 192, 128, 64)


def _shard(dp, ep, slots, a, g, j):
    return (2 * a - g) % ep if j < ((a + 1) * slots) // dp else (g + j + 1) % ep


def _devices(dp, ep, slots, flip):
    return [[a * ep + g for a in range(dp) for g in range(ep) if _shard(dp, ep, slots, a, g, j) == g ^ flip]
            for j in range(slots)]


def _any(me, devices):
    hit = me < 0
    for n in sorted(set(devices)):
        hit = jnp.logical_or(hit, me == n)
    return hit


def _both(src, dests, experts, who, me, buf, rsem, wsem):
    rows = src.shape[1]
    tile = min(buf.shape[2], rows)
    steps = rows // tile
    nbuf = buf.shape[0]

    def read(t):
        return pltpu.make_async_copy(src.at[:, pl.ds(t * tile, tile)],
                                     buf.at[t % nbuf, :, pl.ds(0, tile)], rsem.at[t % nbuf])

    def writes(t, act):
        for j, dest in enumerate(dests):
            if who[j]:
                @pl.when(_any(me, who[j]))
                def _():
                    act(pltpu.make_async_copy(buf.at[t % nbuf, experts[j], pl.ds(0, tile)],
                                              dest(t * tile, tile), wsem.at[t % nbuf, j]))

    ahead = max(1, nbuf - LAG)
    for t in range(min(ahead, steps)):
        read(t).start()
    for t in range(steps):
        read(t).wait()
        writes(t, lambda c: c.start())
        n = t + ahead
        if n < steps:
            if n >= nbuf:
                writes(n - nbuf, lambda c: c.wait())
            read(n).start()
    for t in range(max(0, steps - nbuf), steps):
        writes(t, lambda c: c.wait())


def _one(src, expert, dest, buf, rsem, wsem):
    rows = src.shape[1]
    tile = min(buf.shape[2], rows)
    steps = rows // tile
    nbuf = buf.shape[0]

    def read(t):
        return pltpu.make_async_copy(src.at[expert, pl.ds(t * tile, tile)],
                                     buf.at[t % nbuf, 0, pl.ds(0, tile)], rsem.at[t % nbuf])

    def write(t):
        return pltpu.make_async_copy(buf.at[t % nbuf, 0, pl.ds(0, tile)],
                                     dest(t * tile, tile), wsem.at[t % nbuf, 0])

    ahead = max(1, nbuf - LAG)
    for t in range(min(ahead, steps)):
        read(t).start()
    for t in range(steps):
        read(t).wait()
        write(t).start()
        n = t + ahead
        if n < steps:
            if n >= nbuf:
                write(n - nbuf).wait()
            read(n).start()
    for t in range(max(0, steps - nbuf), steps):
        write(t).wait()


def solution(mesh):
    dp = mesh.shape["dp"]
    ep = mesh.shape["ep"]
    axes = ("dp", "ep")
    any_spec = pl.BlockSpec(memory_space=pltpu.HBM)
    smem_spec = pl.BlockSpec(memory_space=pltpu.SMEM)

    def hand_over(w_gate, w_up, w_down, place):
        wg, wu, wd = w_gate[0], w_up[0], w_down[0]
        n_exp, D, F = wg.shape
        slots = place.shape[1] // (dp * ep)
        own, across, beside, relayed = (_devices(dp, ep, slots, f) for f in (0, 2, 1, 3))
        to_x = [(n ^ 2, n) for n in sorted(set(sum(across, [])) | {m ^ 1 for m in sum(relayed, [])})]
        to_core = [(n ^ 1, n) for n in sorted(set(sum(beside, [])))]
        to_relay = [(n ^ 1, n) for n in sorted(set(sum(relayed, [])))]

        def scratch(cols, tile):
            return [pltpu.VMEM((NBUF, n_exp, tile, cols), jnp.bfloat16),
                    pltpu.SemaphoreType.DMA((NBUF,)), pltpu.SemaphoreType.DMA((NBUF, slots))]

        def where():
            return lax.axis_index("dp") * ep + lax.axis_index("ep")

        def half(out, j, k):
            return lambda r, n: out.at[j, pl.ds(r, n), pl.ds(k * F, F)]

        def rows_of(out, j, first):
            return lambda r, n: out.at[j, pl.ds(first + r, n)]

        def picks(place_ref, me):
            return [lax.rem(place_ref[0, me * slots + j], n_exp) for j in range(slots)]

        def first_kernel(place_ref, g, u, d, cg, cu, cd, o13, o2, buf_f, rf, wf, buf_d, rd, wd_):
            me = where()
            e = picks(place_ref, me)

            @pl.when(_any(me, sum(own, [])))
            def _():
                _both(g, [half(o13, j, 0) for j in range(slots)], e, own, me, buf_f, rf, wf)
                _both(u, [half(o13, j, 1) for j in range(slots)], e, own, me, buf_f, rf, wf)
                _both(d, [rows_of(o2, j, 0) for j in range(slots)], e, own, me, buf_d, rd, wd_)

            for j in range(slots):
                if beside[j]:
                    @pl.when(_any(me, beside[j]))
                    def _():
                        _one(cg, e[j], half(o13, j, 0), buf_f, rf, wf)
                        _one(cu, e[j], half(o13, j, 1), buf_f, rf, wf)
                        _one(cd, e[j], rows_of(o2, j, 0), buf_d, rd, wd_)

        def later_kernel(dest, place_ref, got, rel, _, out, buf, rs, ws):
            me = where()
            e = picks(place_ref, me)

            @pl.when(_any(me, sum(across, [])))
            def _():
                _both(got, [dest(out, j) for j in range(slots)], e, across, me, buf, rs, ws)

            for j in range(slots):
                if relayed[j]:
                    @pl.when(_any(me, relayed[j]))
                    def _():
                        _one(rel, e[j], dest(out, j), buf, rs, ws)

        o13_shape = jax.ShapeDtypeStruct((slots, D, 2 * F), jnp.bfloat16)
        o2_shape = jax.ShapeDtypeStruct((slots, F, D), jnp.bfloat16)

        def later(dest, got, rel, out, tile):
            size = got.size * got.dtype.itemsize
            return pl.pallas_call(
                functools.partial(later_kernel, dest),
                out_shape=jax.ShapeDtypeStruct(out.shape, out.dtype),
                in_specs=[smem_spec, any_spec, any_spec, any_spec], out_specs=any_spec,
                scratch_shapes=scratch(got.shape[2], tile),
                input_output_aliases={3: 0},
                cost_estimate=pl.CostEstimate(flops=0, bytes_accessed=3 * size, transcendentals=0),
            )(place, got, rel, out)

        def permute(x, pairs):
            return lax.ppermute(x, axes, pairs)

        got_g = permute(wg, to_x)
        got_u = permute(wu, to_x)
        pieces, r = [], 0
        for n in DOWN:
            pieces.append((r, permute(lax.slice_in_dim(wd, r, r + n, axis=1), to_x)))
            r += n
        side = [permute(w, to_core) for w in (wg, wu, wd)]
        own_bytes = 2 * 3 * wg.size * wg.dtype.itemsize
        w13, w2 = pl.pallas_call(
            first_kernel, name="place_own",
            out_shape=(o13_shape, o2_shape),
            in_specs=[smem_spec] + [any_spec] * 6, out_specs=(any_spec, any_spec),
            scratch_shapes=scratch(F, TILE) + scratch(D, TILE // 4),
            cost_estimate=pl.CostEstimate(flops=0, bytes_accessed=own_bytes, transcendentals=0),
        )(place, wg, wu, wd, *side)

        for k, got in enumerate((got_g, got_u)):
            w13 = later(functools.partial(lambda k, o, j: half(o, j, k), k),
                        got, permute(got, to_relay), w13, TILE)
        for r, got in pieces:
            w2 = later(functools.partial(lambda r, o, j: rows_of(o, j, r), r),
                       got, permute(got, to_relay), w2, min(TILE // 4, got.shape[1]))
        return w13[None], w2[None]

    spec_in = P(None, "ep", None, None)
    spec_out = P(None, ("dp", "ep"), None, None)
    return jax.shard_map(hand_over, mesh=mesh,
                         in_specs=(spec_in, spec_in, spec_in, P(None, None)),
                         out_specs=(spec_out, spec_out), check_vma=False)
```

time: 1820 us -> 1070 us (0.59)
  the two profiles are of different devices: /device:TPU:0 before, /device:TPU:1 now
where the time goes in v1:
time: 1070 us
  waiting for transfers between devices  842 us (79%)
  Pallas kernels  132 us (12%)
  starting transfers between devices  66.7 us (6%)
  local copies, waits for them, and re-layouts  29.3 us (3%)
    ppermute x17, waiting for transfers between devices, permute(): return lax.ppermute(x, axes, pairs)  842 us
    pallas_call x1, Pallas kernels, hand_over(): pl.pallas_call(first_kernel, name='place_own', out_shape=(o13_shape, o2_s...  67.6 us
    ppermute x17, starting transfers between devices, permute(): return lax.ppermute(x, axes, pairs)  66.7 us
    pallas_call x7, Pallas kernels, later(): pl.pallas_call(functools.partial(later_kernel, dest), out_shape=jax.Shape...  64.4 us
    slice x5, local copies, waits for them, and re-layouts, hand_over(): pieces.append((r, permute(lax.slice_in_dim(wd, r, r + n, axis=1), to_x)))  22.2 us
  transfers between devices with their start and end apart: 17, of which 7 were waited for; matrix products, arithmetic and copies ran while one was open for 2% of the time, Pallas kernels for 11%

profile of v1, /device:TPU:1, one launch (start us, length us, event | category | flops | bytes accessed | tf_op | source)
XLA Modules:
  0.0 1071.3 jit_solution(17536564747107781347)
XLA Ops:
  0.6 3.9 collective-permute-start.2
  7.8 3.4 collective-permute-start.7
  16.2 3.9 slice.22
  20.1 3.4 collective-permute-start.11
  23.5 10.7 slice.24
  34.2 522.1 %collective-permute-done.7.got = bf16[2,64,4096]{2,1,0:T(8,128)(2,1)S(1)} collective-permute-done((bf16[2,64,4096]{2,1,0:T(8,128)(2,1)S(1)}, bf16[2,64,4096]{2,1,0:T(8,128)(2,1)S(1)}, u32[]{:S(2)}, u32[]{:S(2)}) %collective-permute-start.7) | collective-permute-done | bytes 1048608 | tf_op jit(solution)/shard_map/ppermute | solution.py:174
  563.8 15.0 %collective-permute-done.9.got = bf16[2,128,4096]{2,1,0:T(8,128)(2,1)} collective-permute-done((bf16[2,128,4096]{2,1,0:T(8,128)(2,1)}, bf16[2,128,4096]{2,1,0:T(8,128)(2,1)}, u32[]{:S(2)}, u32[]{:S(2)}) %collective-permute-start.9) | collective-permute-done | bytes 2097184 | tf_op jit(solution)/shard_map/ppermute | solution.py:174
  578.8 3.4 collective-permute-start.13
  582.2 30.3 %collective-permute-done.11.got = bf16[2,192,4096]{2,1,0:T(8,128)(2,1)} collective-permute-done((bf16[2,192,4096]{2,1,0:T(8,128)(2,1)}, bf16[2,192,4096]{2,1,0:T(8,128)(2,1)}, u32[]{:S(2)}, u32[]{:S(2)}) %collective-permute-start.11) | collective-permute-done | bytes 3145760 | tf_op jit(solution)/shard_map/ppermute | solution.py:174
  613.8 200.8 %collective-permute-done.13.got = bf16[2,384,4096]{2,1,0:T(8,128)(2,1)S(1)} collective-permute-done((bf16[2,384,4096]{2,1,0:T(8,128)(2,1)S(1)}, bf16[2,384,4096]{2,1,0:T(8,128)(2,1)S(1)}, u32[]{:S(2)}, u32[]{:S(2)}) %collective-permute-start.13) | collective-permute-done | bytes 6291488 | tf_op jit(solution)/shard_map/ppermute | solution.py:174
  817.7 8.0 collective-permute-done.14.rel
  827.0 20.2 %collective-permute-start.3 = (bf16[2,4096,1536]{2,1,0:T(8,128)(2,1)}, bf16[2,4096,1536]{2,1,0:T(8,128)(2,1)}, u32[]{:S(2)}, u32[]{:S(2)}) collective-permute-start(bf16[2,4096,1536]{2,1,0:T(8,128)(2,1)} %collective-permute-done.2.got), channel_id=1, source_target_pairs={{1,0},{3,2}} | collective-permute-start | bytes 75497480 | tf_op jit(solution)/shard_map/ppermute | solution.py:174
  847.2 9.5 collective-permute-start.1
  860.4 31.4 %collective-permute-done.5.cu = bf16[2,4096,1536]{2,1,0:T(8,128)(2,1)} collective-permute-done((bf16[2,4096,1536]{2,1,0:T(8,128)(2,1)}, bf16[2,4096,1536]{2,1,0:T(8,128)(2,1)}, u32[]{:S(2)}, u32[]{:S(2)}) %collective-permute-start.5) | collective-permute-done | bytes 25165856 | tf_op jit(solution)/shard_map/ppermute | solution.py:174
  891.8 3.4 collective-permute-start.10
  895.1 34.7 %collective-permute-done.16.rel = bf16[2,768,4096]{2,1,0:T(8,128)(2,1)S(1)} collective-permute-done((bf16[2,768,4096]{2,1,0:T(8,128)(2,1)S(1)}, bf16[2,768,4096]{2,1,0:T(8,128)(2,1)S(1)}, u32[]{:S(2)}, u32[]{:S(2)}) %collective-permute-start.16) | collective-permute-done | bytes 12582944 | tf_op jit(solution)/shard_map/ppermute | solution.py:174
  929.9 4.5 copy-done.1
  937.6 67.6 %place_own.1 = (bf16[4,4096,3072]{2,1,0:T(8,128)(2,1)}, bf16[4,1536,4096]{2,1,0:T(8,128)(2,1)}) custom-call(s32[1,32]{1,0:T(1,128)} %place_ref.15, bf16[2,4096,1536]{2,1,0:T(8,128)(2,1)} %bitcast.18, bf16[2,4096,1536]{2,1,0:T(8,128)(2,1)} %bitcast.15, bf16[2,1536,4096]{2,1,0:T(8,128)(2,1)} %bitcast.12, bf16[2,4096,1536]{2,1,0:T(8,128)(2,1)} %collective-permute-done.4.cg, ...), custom_call_target="tpu_custom_call" | custom-call | bytes 150994944 | tf_op jit(solution)/shard_map/place_own/pallas_call | solution.py:184
  1005.2 10.6 shard_map.61._
  1015.8 6.6 shard_map.62._
  1024.1 3.9 shard_map.63._
  1028.0 3.6 shard_map.64._
  1034.8 18.2 %shard_map.59._ = bf16[4,4096,3072]{2,1,0:T(8,128)(2,1)} custom-call(s32[1,32]{1,0:T(1,128)} %place_ref.15, bf16[2,4096,1536]{2,1,0:T(8,128)(2,1)} %collective-permute-done.2.got, bf16[2,4096,1536]{2,1,0:T(8,128)(2,1)} %collective-permute-done.3.rel, bf16[4,4096,3072]{2,1,0:T(8,128)(2,1)} %get-tuple-element.4._), custom_call_target="tpu_custom_call", output_to_operand_aliasing={{}: (3, {})} | custom-call | bytes 75497472 | tf_op jit(solution)/shard_map/pallas_call | solution.py:164
  1053.1 18.2 %shard_map.60 = bf16[4,4096,3072]{2,1,0:T(8,128)(2,1)} custom-call(s32[1,32]{1,0:T(1,128)} %place_ref.15, bf16[2,4096,1536]{2,1,0:T(8,128)(2,1)} %collective-permute-done.got, bf16[2,4096,1536]{2,1,0:T(8,128)(2,1)} %collective-permute-done.1.rel, bf16[4,4096,3072]{2,1,0:T(8,128)(2,1)} %shard_map.59._), custom_call_target="tpu_custom_call", output_to_operand_aliasing={{}: (3, {})} | custom-call | bytes 75497472 | tf_op jit(solution)/shard_map/pallas_call | solution.py:164
  (35 shorter events, 33.1 us)
Async XLA Ops:
  0.6 826.4 %collective-permute-start.2 = (bf16[2,4096,1536]{2,1,0:T(8,128)(2,1)}, bf16[2,4096,1536]{2,1,0:T(8,128)(2,1)}, u32[]{:S(2)}, u32[]{:S(2)}) collective-permute-start(bf16[2,4096,1536]{2,1,0:T(8,128)(2,1)} %bitcast.16), channel_id=1, source_target_pairs={{3,1},{1,3},{6,4},{4,6}} | collective-permute-start | bytes 75497480 | tf_op jit(solution)/shard_map/ppermute | solution.py:174
  4.6 842.7 %collective-permute-start = (bf16[2,4096,1536]{2,1,0:T(8,128)(2,1)}, bf16[2,4096,1536]{2,1,0:T(8,128)(2,1)}, u32[]{:S(2)}, u32[]{:S(2)}) collective-permute-start(bf16[2,4096,1536]{2,1,0:T(8,128)(2,1)} %bitcast.13), channel_id=1, source_target_pairs={{3,1},{1,3},{6,4},{4,6}} | collective-permute-start | bytes 75497480 | tf_op jit(solution)/shard_map/ppermute | solution.py:174
  7.8 548.4 %collective-permute-start.7 = (bf16[2,64,4096]{2,1,0:T(8,128)(2,1)S(1)}, bf16[2,64,4096]{2,1,0:T(8,128)(2,1)S(1)}, u32[]{:S(2)}, u32[]{:S(2)}) collective-permute-start(bf16[2,64,4096]{2,1,0:T(8,128)(2,1)S(1)} %slice.20), channel_id=1, source_target_pairs={{3,1},{1,3},{6,4},{4,6}} | collective-permute-start | bytes 3145736 | tf_op jit(solution)/shard_map/ppermute | solution.py:174
  14.3 564.5 %collective-permute-start.9 = (bf16[2,128,4096]{2,1,0:T(8,128)(2,1)}, bf16[2,128,4096]{2,1,0:T(8,128)(2,1)}, u32[]{:S(2)}, u32[]{:S(2)}) collective-permute-start(bf16[2,128,4096]{2,1,0:T(8,128)(2,1)} %slice.21), channel_id=1, source_target_pairs={{3,1},{1,3},{6,4},{4,6}} | collective-permute-start | bytes 6291464 | tf_op jit(solution)/shard_map/ppermute | solution.py:174
  20.1 592.4 %collective-permute-start.11 = (bf16[2,192,4096]{2,1,0:T(8,128)(2,1)}, bf16[2,192,4096]{2,1,0:T(8,128)(2,1)}, u32[]{:S(2)}, u32[]{:S(2)}) collective-permute-start(bf16[2,192,4096]{2,1,0:T(8,128)(2,1)} %slice.22), channel_id=1, source_target_pairs={{3,1},{1,3},{6,4},{4,6}} | collective-permute-start | bytes 9437192 | tf_op jit(solution)/shard_map/ppermute | solution.py:174
  556.3 1.0 copy-start.5
  557.2 259.1 %collective-permute-start.15 = (bf16[2,768,4096]{2,1,0:T(8,128)(2,1)}, bf16[2,768,4096]{2,1,0:T(8,128)(2,1)S(1)}, u32[]{:S(2)}, u32[]{:S(2)}) collective-permute-start(bf16[2,768,4096]{2,1,0:T(8,128)(2,1)} %slice.24), channel_id=1, source_target_pairs={{3,1},{1,3},{6,4},{4,6}} | collective-permute-start | bytes 37748744 | tf_op jit(solution)/shard_map/ppermute | solution.py:174
  578.8 235.8 %collective-permute-start.13 = (bf16[2,384,4096]{2,1,0:T(8,128)(2,1)S(1)}, bf16[2,384,4096]{2,1,0:T(8,128)(2,1)S(1)}, u32[]{:S(2)}, u32[]{:S(2)}) collective-permute-start(bf16[2,384,4096]{2,1,0:T(8,128)(2,1)S(1)} %slice.23), channel_id=1, source_target_pairs={{3,1},{1,3},{6,4},{4,6}} | collective-permute-start | bytes 18874376 | tf_op jit(solution)/shard_map/ppermute | solution.py:174
  612.5 244.2 %collective-permute-start.6 = (bf16[2,1536,4096]{2,1,0:T(8,128)(2,1)}, bf16[2,1536,4096]{2,1,0:T(8,128)(2,1)}, u32[]{:S(2)}, u32[]{:S(2)}) collective-permute-start(bf16[2,1536,4096]{2,1,0:T(8,128)(2,1)} %bitcast.11), channel_id=1, source_target_pairs={{0,1},{2,3}} | collective-permute-start | bytes 75497480 | tf_op jit(solution)/shard_map/ppermute | solution.py:174
  814.7 42.1 %copy-start.2 = (bf16[2,384,4096]{2,1,0:T(8,128)(2,1)}, bf16[2,384,4096]{2,1,0:T(8,128)(2,1)S(1)}, u32[]{:S(2)}) copy-start(bf16[2,384,4096]{2,1,0:T(8,128)(2,1)S(1)} %collective-permute-done.13.got) | copy-start | bytes 18874372
  814.7 11.1 %collective-permute-start.14 = (bf16[2,384,4096]{2,1,0:T(8,128)(2,1)S(1)}, bf16[2,384,4096]{2,1,0:T(8,128)(2,1)S(1)}, u32[]{:S(2)}, u32[]{:S(2)}) collective-permute-start(bf16[2,384,4096]{2,1,0:T(8,128)(2,1)S(1)} %collective-permute-done.13.got), channel_id=1, source_target_pairs={{1,0},{3,2}} | collective-permute-start | bytes 18874376 | tf_op jit(solution)/shard_map/ppermute | solution.py:174
  816.4 40.4 %copy-start = (bf16[2,768,4096]{2,1,0:T(8,128)(2,1)}, bf16[2,768,4096]{2,1,0:T(8,128)(2,1)S(1)}, u32[]{:S(2)}) copy-start(bf16[2,768,4096]{2,1,0:T(8,128)(2,1)S(1)} %collective-permute-done.15.got) | copy-start | bytes 37748740
  816.4 42.5 %collective-permute-start.4 = (bf16[2,4096,1536]{2,1,0:T(8,128)(2,1)}, bf16[2,4096,1536]{2,1,0:T(8,128)(2,1)}, u32[]{:S(2)}, u32[]{:S(2)}) collective-permute-start(bf16[2,4096,1536]{2,1,0:T(8,128)(2,1)} %bitcast.17), channel_id=1, source_target_pairs={{0,1},{2,3}} | collective-permute-start | bytes 75497480 | tf_op jit(solution)/shard_map/ppermute | solution.py:174
  825.7 31.0 %copy-start.3 = (bf16[2,384,4096]{2,1,0:T(8,128)(2,1)}, bf16[2,384,4096]{2,1,0:T(8,128)(2,1)S(1)}, u32[]{:S(2)}) copy-start(bf16[2,384,4096]{2,1,0:T(8,128)(2,1)S(1)} %collective-permute-done.14.rel) | copy-start | bytes 18874372
  825.7 66.0 %collective-permute-start.5 = (bf16[2,4096,1536]{2,1,0:T(8,128)(2,1)}, bf16[2,4096,1536]{2,1,0:T(8,128)(2,1)}, u32[]{:S(2)}, u32[]{:S(2)}) collective-permute-start(bf16[2,4096,1536]{2,1,0:T(8,128)(2,1)} %bitcast.14), channel_id=1, source_target_pairs={{0,1},{2,3}} | collective-permute-start | bytes 75497480 | tf_op jit(solution)/shard_map/ppermute | solution.py:174
  827.0 207.8 %collective-permute-start.3 = (bf16[2,4096,1536]{2,1,0:T(8,128)(2,1)}, bf16[2,4096,1536]{2,1,0:T(8,128)(2,1)}, u32[]{:S(2)}, u32[]{:S(2)}) collective-permute-start(bf16[2,4096,1536]{2,1,0:T(8,128)(2,1)} %collective-permute-done.2.got), channel_id=1, source_target_pairs={{1,0},{3,2}} | collective-permute-start | bytes 75497480 | tf_op jit(solution)/shard_map/ppermute | solution.py:174
  847.2 205.8 %collective-permute-start.1 = (bf16[2,4096,1536]{2,1,0:T(8,128)(2,1)}, bf16[2,4096,1536]{2,1,0:T(8,128)(2,1)}, u32[]{:S(2)}, u32[]{:S(2)}) collective-permute-start(bf16[2,4096,1536]{2,1,0:T(8,128)(2,1)} %collective-permute-done.got), channel_id=1, source_target_pairs={{1,0},{3,2}} | collective-permute-start | bytes 75497480 | tf_op jit(solution)/shard_map/ppermute | solution.py:174
  856.8 73.1 %collective-permute-start.16 = (bf16[2,768,4096]{2,1,0:T(8,128)(2,1)S(1)}, bf16[2,768,4096]{2,1,0:T(8,128)(2,1)S(1)}, u32[]{:S(2)}, u32[]{:S(2)}) collective-permute-start(bf16[2,768,4096]{2,1,0:T(8,128)(2,1)S(1)} %collective-permute-done.15.got), channel_id=1, source_target_pairs={{1,0},{3,2}} | collective-permute-start | bytes 37748744 | tf_op jit(solution)/shard_map/ppermute | solution.py:174
  858.9 163.5 %collective-permute-start.12 = (bf16[2,192,4096]{2,1,0:T(8,128)(2,1)}, bf16[2,192,4096]{2,1,0:T(8,128)(2,1)S(1)}, u32[]{:S(2)}, u32[]{:S(2)}) collective-permute-start(bf16[2,192,4096]{2,1,0:T(8,128)(2,1)} %collective-permute-done.11.got), channel_id=1, source_target_pairs={{1,0},{3,2}} | collective-permute-start | bytes 9437192 | tf_op jit(solution)/shard_map/ppermute | solution.py:174
  891.8 136.2 %collective-permute-start.10 = (bf16[2,128,4096]{2,1,0:T(8,128)(2,1)}, bf16[2,128,4096]{2,1,0:T(8,128)(2,1)}, u32[]{:S(2)}, u32[]{:S(2)}) collective-permute-start(bf16[2,128,4096]{2,1,0:T(8,128)(2,1)} %collective-permute-done.9.got), channel_id=1, source_target_pairs={{1,0},{3,2}} | collective-permute-start | bytes 6291464 | tf_op jit(solution)/shard_map/ppermute | solution.py:174
  929.9 4.5 copy-start.1
  934.4 97.2 %collective-permute-start.8 = (bf16[2,64,4096]{2,1,0:T(8,128)(2,1)}, bf16[2,64,4096]{2,1,0:T(8,128)(2,1)}, u32[]{:S(2)}, u32[]{:S(2)}) collective-permute-start(bf16[2,64,4096]{2,1,0:T(8,128)(2,1)} %copy-done.5), channel_id=1, source_target_pairs={{1,0},{3,2}} | collective-permute-start | bytes 3145736 | tf_op jit(solution)/shard_map/ppermute | solution.py:174
  1022.4 1.6 copy-start.4

commit v2 on v1

v2 whole, which is shorter than its diff:
```python
import functools

import jax
import jax.numpy as jnp
from jax import lax
from jax.experimental import pallas as pl
from jax.experimental.pallas import tpu as pltpu
from jax.sharding import PartitionSpec as P


TILE = 256
NBUF = 8
LAG = 3
VMEM_LIMIT = 32 * 1024 * 1024
BOTH_ROWS = 768
LAST_ROWS = (576, 128, 64)


def _shard(dp, ep, slots, a, g, j):
    return (2 * a - g) % ep if j < ((a + 1) * slots) // dp else (g + j + 1) % ep


def _devices(dp, ep, slots, flip):
    return [[a * ep + g for a in range(dp) for g in range(ep) if _shard(dp, ep, slots, a, g, j) == g ^ flip]
            for j in range(slots)]


def _any(me, devices):
    hit = me < 0
    for n in sorted(set(devices)):
        hit = jnp.logical_or(hit, me == n)
    return hit


def _stream(steps, nbuf, read, writes):
    ahead = max(1, nbuf - LAG)
    for t in range(min(ahead, steps)):
        read(t).start()
    for t in range(steps):
        read(t).wait()
        writes(t, lambda c: c.start())
        n = t + ahead
        if n < steps:
            if n >= nbuf:
                writes(n - nbuf, lambda c: c.wait())
            read(n).start()
    for t in range(max(0, steps - nbuf), steps):
        writes(t, lambda c: c.wait())


def _both(src, dests, experts, who, me, buf, rsem, wsem):
    rows, nbuf = src.shape[1], buf.shape[0]
    tile = min(buf.shape[2], rows)

    def read(t):
        return pltpu.make_async_copy(src.at[:, pl.ds(t * tile, tile)],
                                     buf.at[t % nbuf, :, pl.ds(0, tile)], rsem.at[t % nbuf])

    def writes(t, act):
        for j, dest in enumerate(dests):
            if who[j]:
                @pl.when(_any(me, who[j]))
                def _():
                    act(pltpu.make_async_copy(buf.at[t % nbuf, experts[j], pl.ds(0, tile)],
                                              dest(t * tile, tile), wsem.at[t % nbuf, j]))

    _stream(rows // tile, nbuf, read, writes)


def _one(src, dests, wanted, buf, rsem, wsem):
    rows, nbuf = src.shape[0], buf.shape[0]
    tile = min(buf.shape[2], rows)

    def read(t):
        return pltpu.make_async_copy(src.at[pl.ds(t * tile, tile)],
                                     buf.at[t % nbuf, 0, pl.ds(0, tile)], rsem.at[t % nbuf])

    def writes(t, act):
        for j, dest in enumerate(dests):
            def go():
                act(pltpu.make_async_copy(buf.at[t % nbuf, 0, pl.ds(0, tile)],
                                          dest(t * tile, tile), wsem.at[t % nbuf, j]))

            if wanted[j] is True:
                go()
            elif wanted[j] is not None:
                pl.when(wanted[j])(go)

    _stream(rows // tile, nbuf, read, writes)


def solution(mesh):
    dp = mesh.shape["dp"]
    ep = mesh.shape["ep"]
    axes = ("dp", "ep")
    hbm = pl.BlockSpec(memory_space=pltpu.HBM)
    vmem = pl.BlockSpec(memory_space=pltpu.VMEM)
    smem = pl.BlockSpec(memory_space=pltpu.SMEM)

    def hand_over(w_gate, w_up, w_down, place):
        wg, wu, wd = w_gate[0], w_up[0], w_down[0]
        n_exp, D, F = wg.shape
        slots = place.shape[1] // (dp * ep)
        own, across, beside, relayed = (_devices(dp, ep, slots, f) for f in (0, 2, 1, 3))
        to_x = [(n ^ 2, n) for n in sorted(set(sum(across, [])) | {m ^ 1 for m in sum(relayed, [])})]
        to_core = [(n ^ 1, n) for n in sorted(set(sum(beside, [])))]
        to_relay = [(n ^ 1, n) for n in sorted(set(sum(relayed, [])))]

        def ring(cols, tile, experts=n_exp):
            return [pltpu.VMEM((NBUF, experts, tile, cols), jnp.bfloat16),
                    pltpu.SemaphoreType.DMA((NBUF,)), pltpu.SemaphoreType.DMA((NBUF, slots))]

        def where():
            return lax.axis_index("dp") * ep + lax.axis_index("ep")

        def half(out, j, k):
            return lambda r, n: out.at[j, pl.ds(r, n), pl.ds(k * F, F)]

        def rows_of(out, j, first):
            return lambda r, n: out.at[j, pl.ds(first + r, n)]

        def picks(place_ref, me):
            return [lax.rem(place_ref[0, me * slots + j], n_exp) for j in range(slots)]

        def early(place_ref, me, flip):
            e = me * 0
            for j in range(slots):
                for n in relayed[j]:
                    e = jnp.where(me == n ^ flip, lax.rem(place_ref[0, n * slots + j], n_exp), e)
            return e

        def call(kernel, out_shape, in_specs, scratch, size, aliases=None):
            return pl.pallas_call(
                kernel, out_shape=out_shape, in_specs=in_specs,
                out_specs=jax.tree.map(lambda _: hbm, out_shape), scratch_shapes=scratch,
                input_output_aliases=aliases or {},
                compiler_params=pltpu.CompilerParams(vmem_limit_bytes=VMEM_LIMIT),
                cost_estimate=pl.CostEstimate(flops=0, bytes_accessed=size, transcendentals=0))

        def own_kernel(place_ref, g, u, d, cg, cu, cd, o13, o2, buf_f, rf, wf, buf_d, rd, wd_):
            me = where()
            e = picks(place_ref, me)

            @pl.when(_any(me, sum(own, [])))
            def _():
                _both(g, [half(o13, j, 0) for j in range(slots)], e, own, me, buf_f, rf, wf)
                _both(u, [half(o13, j, 1) for j in range(slots)], e, own, me, buf_f, rf, wf)
                _both(d, [rows_of(o2, j, 0) for j in range(slots)], e, own, me, buf_d, rd, wd_)

            for j in range(slots):
                if beside[j]:
                    @pl.when(_any(me, beside[j]))
                    def _():
                        _one(cg.at[e[j]], [half(o13, j, 0)], [True], buf_f, rf, wf)
                        _one(cu.at[e[j]], [half(o13, j, 1)], [True], buf_f, rf, wf)
                        _one(cd.at[e[j]], [rows_of(o2, j, 0)], [True], buf_d, rd, wd_)

        def both_kernel(dest, place_ref, got, rel, _, out, buf, rs, ws):
            me = where()
            e = picks(place_ref, me)

            @pl.when(_any(me, sum(across, [])))
            def _():
                _both(got, [dest(out, j) for j in range(slots)], e, across, me, buf, rs, ws)

            for j in range(slots):
                if relayed[j]:
                    @pl.when(_any(me, relayed[j]))
                    def _():
                        _one(rel.at[e[j]], [dest(out, j)], [True], buf, rs, ws)

        def wants(place_ref, me, first):
            e, a = picks(place_ref, me), early(place_ref, me, 1)
            return [jnp.logical_and(_any(me, across[j]), (e[j] == a) == first) if across[j] else None
                    for j in range(slots)]

        def first_kernel(dest, place_ref, got, rel, _, out, buf, rs, ws):
            me = where()

            @pl.when(_any(me, sum(across, [])))
            def _():
                _one(got, [dest(out, j) for j in range(slots)], wants(place_ref, me, True), buf, rs, ws)

            for j in range(slots):
                if relayed[j]:
                    @pl.when(_any(me, relayed[j]))
                    def _():
                        copy = pltpu.make_async_copy(rel, dest(out, j)(0, rel.shape[0]), rs.at[0])
                        copy.start()
                        copy.wait()

        def last_kernel(dest, place_ref, got, _, out, ws):
            want = wants(place_ref, where(), False)
            for act in (lambda c: c.start(), lambda c: c.wait()):
                for j in range(slots):
                    if want[j] is not None:
                        @pl.when(want[j])
                        def _():
                            act(pltpu.make_async_copy(got, dest(out, j)(0, got.shape[0]), ws.at[j]))

        def cut_kernel(place_ref, d, both, first, *rest):
            lasts, (buf, rs, ws) = rest[:-3], rest[-3:]
            e = early(place_ref, where(), 3)
            tile = buf.shape[2]
            steps = []
            for x in range(n_exp):
                for r in range(0, BOTH_ROWS, tile):
                    steps.append((d.at[x, pl.ds(r, tile)], both.at[x, pl.ds(r, tile)], tile))
            for ex, outs in ((e, [first]), (1 - e, lasts)):
                r = BOTH_ROWS
                for o in outs:
                    for q in range(0, o.shape[0], tile):
                        n = min(tile, o.shape[0] - q)
                        steps.append((d.at[ex, pl.ds(r + q, n)], o.at[pl.ds(q, n)], n))
                    r += o.shape[0]

            def read(t):
                return pltpu.make_async_copy(steps[t][0], buf.at[t % NBUF, 0, pl.ds(0, steps[t][2])], rs.at[t % NBUF])

            def writes(t, act):
                act(pltpu.make_async_copy(buf.at[t % NBUF, 0, pl.ds(0, steps[t][2])], steps[t][1], ws.at[t % NBUF, 0]))

            _stream(len(steps), NBUF, read, writes)

        def permute(x, pairs):
            return lax.ppermute(x, axes, pairs)

        def shape(*dims):
            return jax.ShapeDtypeStruct(dims, jnp.bfloat16)

        block = wg.size * wg.dtype.itemsize
        got_g = permute(wg, to_x)
        got_u = permute(wu, to_x)
        cuts = call(cut_kernel,
                    [shape(n_exp, BOTH_ROWS, D), shape(F - BOTH_ROWS, D)] + [shape(n, D) for n in LAST_ROWS],
                    [smem, hbm], ring(D, TILE // 2, 1), 2 * block)(place, wd)
        got_d = [permute(c, to_x) for c in cuts]
        side = [permute(w, to_core) for w in (wg, wu, wd)]
        w13, w2 = call(own_kernel, (shape(slots, D, 2 * F), shape(slots, F, D)),
                       [smem] + [hbm] * 6, ring(F, TILE) + ring(D, TILE // 4), 6 * block)(place, wg, wu, wd, *side)

        def later(kernel, dest, got, out, cols, tile, rel_in=hbm):
            rel = permute(got, to_relay)
            return call(functools.partial(kernel, dest), shape(*out.shape), [smem, hbm, rel_in, hbm],
                        ring(cols, tile), 3 * got.size * 2, {3: 0})(place, got, rel, out)

        w13 = later(both_kernel, lambda o, j: half(o, j, 0), got_g, w13, F, TILE)
        w13 = later(both_kernel, lambda o, j: half(o, j, 1), got_u, w13, F, TILE)
        w2 = later(both_kernel, lambda o, j: rows_of(o, j, 0), got_d[0], w2, D, TILE // 4)
        w2 = later(first_kernel, lambda o, j: rows_of(o, j, BOTH_ROWS), got_d[1], w2, D, TILE // 2,
                   vmem)
        r = BOTH_ROWS
        for got in got_d[2:]:
            w2 = call(functools.partial(last_kernel, lambda o, j, r=r: rows_of(o, j, r)),
                      shape(*w2.shape), [smem, vmem, hbm], [pltpu.SemaphoreType.DMA((slots,))],
                      3 * got.size * 2, {2: 0})(place, got, w2)
            r += got.shape[0]
        return w13[None], w2[None]

    spec_in = P(None, "ep", None, None)
    spec_out = P(None, ("dp", "ep"), None, None)
    return jax.shard_map(hand_over, mesh=mesh,
                         in_specs=(spec_in, spec_in, spec_in, P(None, None)),
                         out_specs=(spec_out, spec_out), check_vma=False)
```

time: 1070 us -> 984 us (0.920)
  waiting for transfers between devices: 842 us -> 785 us
  local copies, waits for them, and re-layouts: 29.3 us -> 2.79 us
    ppermute x17 -> x14, waiting for transfers between devices: 842 us -> 785 us  [permute(): return lax.ppermute(x, axes, pairs)]
    slice x5 -> x0, local copies, waits for them, and re-layouts: 22.2 us -> none  [hand_over(): pieces.append((r, permute(lax.slice_in_dim(wd, r, r + n, axis=1), to_x)))]
    ppermute x17 -> x14, starting transfers between devices: 66.7 us -> 62.4 us  [permute(): return lax.ppermute(x, axes, pairs)]
    pallas_call x8 -> x9, Pallas kernels: 132 us -> 133 us  [the longest x1 67.5 us: hand_over(): call(own_kernel, (shape(slots, D, 2 * F), shape(slots, F, D)), [smem] + [...]
  transfers between devices with their start and end apart: 17 -> 14, of which waited for: 7 -> 4; matrix products, arithmetic and copies ran while one was open for 2% -> 0% of each run, Pallas kernels for 11% -> 12%
where the time goes in v2:
time: 984 us; the launch traced here: 983 us
  waiting for transfers between devices  785 us (80%)
  Pallas kernels  133 us (14%)
  starting transfers between devices  62.4 us (6%)
    ppermute x14, waiting for transfers between devices, permute(): return lax.ppermute(x, axes, pairs)  785 us
    pallas_call x1, Pallas kernels, hand_over(): call(own_kernel, (shape(slots, D, 2 * F), shape(slots, F, D)), [smem] + [...  67.5 us
    ppermute x14, starting transfers between devices, permute(): return lax.ppermute(x, axes, pairs)  62.4 us
    pallas_call x4, Pallas kernels, later(): call(functools.partial(kernel, dest), shape(*out.shape), [smem, hbm, rel_...  47.9 us
  transfers between devices with their start and end apart: 14, of which 4 were waited for; matrix products, arithmetic and copies ran while one was open for 0% of the time, Pallas kernels for 12%

profile of v2, /device:TPU:1, one launch (start us, length us, event | category | flops | bytes accessed | tf_op | source)
XLA Modules:
  0.0 983.4 jit_solution(7575226810393492774)
XLA Ops:
  0.6 3.9 collective-permute-start.2
  4.6 1.9 collective-permute-start
  7.2 14.9 %shard_map.62 = (bf16[2,768,4096]{2,1,0:T(8,128)(2,1)}, bf16[768,4096]{1,0:T(8,128)(2,1)S(1)}, bf16[576,4096]{1,0:T(8,128)(2,1)S(1)}, bf16[128,4096]{1,0:T(8,128)(2,1)S(1)}, bf16[64,4096]{1,0:T(8,128)(2,1)}) custom-call(s32[1,32]{1,0:T(1,128)S(1)} %copy-done, bf16[2,1536,4096]{2,1,0:T(8,128)(2,1)} %bitcast.6), custom_call_target="tpu_custom_call" | custom-call | bytes 50331648 | tf_op jit(solution)/shard_map/pallas_call | solution.py:234
  22.1 2.1 copy-done.1
  24.3 3.3 collective-permute-start.12
  27.6 1.9 collective-permute-start.10
  29.5 1.3 collective-permute-start.4
  30.8 716.4 %collective-permute-done.10.got = bf16[768,4096]{1,0:T(8,128)(2,1)S(1)} collective-permute-done((bf16[768,4096]{1,0:T(8,128)(2,1)S(1)}, bf16[768,4096]{1,0:T(8,128)(2,1)S(1)}, u32[]{:S(2)}, u32[]{:S(2)}) %collective-permute-start.10) | collective-permute-done | bytes 6291488 | tf_op jit(solution)/shard_map/ppermute | solution.py:226
  747.3 1.7 collective-permute-start.11
  749.0 1.3 collective-permute-start.5
  750.3 8.1 collective-permute-done.11.rel
  759.6 19.9 %collective-permute-start.3 = (bf16[2,4096,1536]{2,1,0:T(8,128)(2,1)}, bf16[2,4096,1536]{2,1,0:T(8,128)(2,1)}, u32[]{:S(2)}, u32[]{:S(2)}) collective-permute-start(bf16[2,4096,1536]{2,1,0:T(8,128)(2,1)} %collective-permute-done.2.got), channel_id=1, source_target_pairs={{1,0},{3,2}} | collective-permute-start | bytes 75497480 | tf_op jit(solution)/shard_map/ppermute | solution.py:226
  779.5 9.5 collective-permute-start.1
  789.0 6.3 collective-permute-start.13
  795.3 3.4 collective-permute-start.9
  798.6 25.7 %collective-permute-done.6.cd = bf16[2,1536,4096]{2,1,0:T(8,128)(2,1)} collective-permute-done((bf16[2,1536,4096]{2,1,0:T(8,128)(2,1)}, bf16[2,1536,4096]{2,1,0:T(8,128)(2,1)}, u32[]{:S(2)}, u32[]{:S(2)}) %collective-permute-start.6) | collective-permute-done | bytes 25165856 | tf_op jit(solution)/shard_map/ppermute | solution.py:226
  824.3 3.4 collective-permute-start.8
  827.7 34.5 %collective-permute-done.13.rel = bf16[2,768,4096]{2,1,0:T(8,128)(2,1)} collective-permute-done((bf16[2,768,4096]{2,1,0:T(8,128)(2,1)S(1)}, bf16[2,768,4096]{2,1,0:T(8,128)(2,1)}, u32[]{:S(2)}, u32[]{:S(2)}) %collective-permute-start.13) | collective-permute-done | bytes 12582944 | tf_op jit(solution)/shard_map/ppermute | solution.py:226
  862.2 3.4 collective-permute-start.7
  865.6 67.5 %shard_map.59 = (bf16[4,4096,3072]{2,1,0:T(8,128)(2,1)}, bf16[4,1536,4096]{2,1,0:T(8,128)(2,1)}) custom-call(s32[1,32]{1,0:T(1,128)S(1)} %copy-done, bf16[2,4096,1536]{2,1,0:T(8,128)(2,1)} %bitcast.14, bf16[2,4096,1536]{2,1,0:T(8,128)(2,1)} %bitcast.11, bf16[2,1536,4096]{2,1,0:T(8,128)(2,1)} %bitcast.8, bf16[2,4096,1536]{2,1,0:T(8,128)(2,1)} %copy-done.2, ...), custom_call_target="tpu_custom_call" | custom-call | bytes 150994944 | tf_op jit(solution)/shard_map/pallas_call | solution.py:239
  933.1 5.8 shard_map.63._
  938.9 5.8 shard_map.64._
  947.2 18.1 %shard_map.60._ = bf16[4,4096,3072]{2,1,0:T(8,128)(2,1)} custom-call(s32[1,32]{1,0:T(1,128)S(1)} %copy-done, bf16[2,4096,1536]{2,1,0:T(8,128)(2,1)} %collective-permute-done.2.got, bf16[2,4096,1536]{2,1,0:T(8,128)(2,1)} %collective-permute-done.3.rel, bf16[4,4096,3072]{2,1,0:T(8,128)(2,1)} %get-tuple-element.9._), custom_call_target="tpu_custom_call", output_to_operand_aliasing={{}: (3, {})} | custom-call | bytes 75497472 | tf_op jit(solution)/shard_map/pallas_call | solution.py:244
  965.3 18.1 %shard_map.61 = bf16[4,4096,3072]{2,1,0:T(8,128)(2,1)} custom-call(s32[1,32]{1,0:T(1,128)S(1)} %copy-done, bf16[2,4096,1536]{2,1,0:T(8,128)(2,1)} %collective-permute-done.got, bf16[2,4096,1536]{2,1,0:T(8,128)(2,1)} %collective-permute-done.1.rel, bf16[4,4096,3072]{2,1,0:T(8,128)(2,1)} %shard_map.60._), custom_call_target="tpu_custom_call", output_to_operand_aliasing={{}: (3, {})} | custom-call | bytes 75497472 | tf_op jit(solution)/shard_map/pallas_call | solution.py:244
  (19 shorter events, 4.3 us)
Async XLA Ops:
  0.6 759.0 %collective-permute-start.2 = (bf16[2,4096,1536]{2,1,0:T(8,128)(2,1)}, bf16[2,4096,1536]{2,1,0:T(8,128)(2,1)}, u32[]{:S(2)}, u32[]{:S(2)}) collective-permute-start(bf16[2,4096,1536]{2,1,0:T(8,128)(2,1)} %bitcast.12), channel_id=1, source_target_pairs={{3,1},{1,3},{6,4},{4,6}} | collective-permute-start | bytes 75497480 | tf_op jit(solution)/shard_map/ppermute | solution.py:226
  4.6 774.9 %collective-permute-start = (bf16[2,4096,1536]{2,1,0:T(8,128)(2,1)}, bf16[2,4096,1536]{2,1,0:T(8,128)(2,1)}, u32[]{:S(2)}, u32[]{:S(2)}) collective-permute-start(bf16[2,4096,1536]{2,1,0:T(8,128)(2,1)} %bitcast.9), channel_id=1, source_target_pairs={{3,1},{1,3},{6,4},{4,6}} | collective-permute-start | bytes 75497480 | tf_op jit(solution)/shard_map/ppermute | solution.py:226
  6.5 0.7 copy-start
  22.1 2.1 copy-start.1
  24.3 724.7 %collective-permute-start.12 = (bf16[2,768,4096]{2,1,0:T(8,128)(2,1)}, bf16[2,768,4096]{2,1,0:T(8,128)(2,1)S(1)}, u32[]{:S(2)}, u32[]{:S(2)}) collective-permute-start(bf16[2,768,4096]{2,1,0:T(8,128)(2,1)} %get-tuple-element.14), channel_id=1, source_target_pairs={{3,1},{1,3},{6,4},{4,6}} | collective-permute-start | bytes 37748744 | tf_op jit(solution)/shard_map/ppermute | solution.py:226
  27.6 719.7 %collective-permute-start.10 = (bf16[768,4096]{1,0:T(8,128)(2,1)S(1)}, bf16[768,4096]{1,0:T(8,128)(2,1)S(1)}, u32[]{:S(2)}, u32[]{:S(2)}) collective-permute-start(bf16[768,4096]{1,0:T(8,128)(2,1)S(1)} %get-tuple-element.13), channel_id=1, source_target_pairs={{3,1},{1,3},{6,4},{4,6}} | collective-permute-start | bytes 18874376 | tf_op jit(solution)/shard_map/ppermute | solution.py:226
  29.5 759.5 %collective-permute-start.4 = (bf16[2,4096,1536]{2,1,0:T(8,128)(2,1)}, bf16[2,4096,1536]{2,1,0:T(8,128)(2,1)S(1)}, u32[]{:S(2)}, u32[]{:S(2)}) collective-permute-start(bf16[2,4096,1536]{2,1,0:T(8,128)(2,1)} %bitcast.13), channel_id=1, source_target_pairs={{0,1},{2,3}} | collective-permute-start | bytes 75497480 | tf_op jit(solution)/shard_map/ppermute | solution.py:226
  747.3 11.1 %collective-permute-start.11 = (bf16[768,4096]{1,0:T(8,128)(2,1)S(1)}, bf16[768,4096]{1,0:T(8,128)(2,1)S(1)}, u32[]{:S(2)}, u32[]{:S(2)}) collective-permute-start(bf16[768,4096]{1,0:T(8,128)(2,1)S(1)} %collective-permute-done.10.got), channel_id=1, source_target_pairs={{1,0},{3,2}} | collective-permute-start | bytes 18874376 | tf_op jit(solution)/shard_map/ppermute | solution.py:226
  749.0 46.3 %collective-permute-start.5 = (bf16[2,4096,1536]{2,1,0:T(8,128)(2,1)}, bf16[2,4096,1536]{2,1,0:T(8,128)(2,1)}, u32[]{:S(2)}, u32[]{:S(2)}) collective-permute-start(bf16[2,4096,1536]{2,1,0:T(8,128)(2,1)} %bitcast.10), channel_id=1, source_target_pairs={{0,1},{2,3}} | collective-permute-start | bytes 75497480 | tf_op jit(solution)/shard_map/ppermute | solution.py:226
  758.3 66.0 %collective-permute-start.6 = (bf16[2,1536,4096]{2,1,0:T(8,128)(2,1)}, bf16[2,1536,4096]{2,1,0:T(8,128)(2,1)}, u32[]{:S(2)}, u32[]{:S(2)}) collective-permute-start(bf16[2,1536,4096]{2,1,0:T(8,128)(2,1)} %bitcast.7), channel_id=1, source_target_pairs={{0,1},{2,3}} | collective-permute-start | bytes 75497480 | tf_op jit(solution)/shard_map/ppermute | solution.py:226
  759.6 187.6 %collective-permute-start.3 = (bf16[2,4096,1536]{2,1,0:T(8,128)(2,1)}, bf16[2,4096,1536]{2,1,0:T(8,128)(2,1)}, u32[]{:S(2)}, u32[]{:S(2)}) collective-permute-start(bf16[2,4096,1536]{2,1,0:T(8,128)(2,1)} %collective-permute-done.2.got), channel_id=1, source_target_pairs={{1,0},{3,2}} | collective-permute-start | bytes 75497480 | tf_op jit(solution)/shard_map/ppermute | solution.py:226
  779.5 185.8 %collective-permute-start.1 = (bf16[2,4096,1536]{2,1,0:T(8,128)(2,1)}, bf16[2,4096,1536]{2,1,0:T(8,128)(2,1)}, u32[]{:S(2)}, u32[]{:S(2)}) collective-permute-start(bf16[2,4096,1536]{2,1,0:T(8,128)(2,1)} %collective-permute-done.got), channel_id=1, source_target_pairs={{1,0},{3,2}} | collective-permute-start | bytes 75497480 | tf_op jit(solution)/shard_map/ppermute | solution.py:226
  789.0 73.2 %copy-start.2 = (bf16[2,4096,1536]{2,1,0:T(8,128)(2,1)}, bf16[2,4096,1536]{2,1,0:T(8,128)(2,1)S(1)}, u32[]{:S(2)}) copy-start(bf16[2,4096,1536]{2,1,0:T(8,128)(2,1)S(1)} %collective-permute-done.4.cg) | copy-start | bytes 75497472
  789.0 73.2 %collective-permute-start.13 = (bf16[2,768,4096]{2,1,0:T(8,128)(2,1)S(1)}, bf16[2,768,4096]{2,1,0:T(8,128)(2,1)}, u32[]{:S(2)}, u32[]{:S(2)}) collective-permute-start(bf16[2,768,4096]{2,1,0:T(8,128)(2,1)S(1)} %collective-permute-done.12.got), channel_id=1, source_target_pairs={{1,0},{3,2}} | collective-permute-start | bytes 37748744 | tf_op jit(solution)/shard_map/ppermute | solution.py:226
  795.3 149.5 %collective-permute-start.9 = (bf16[576,4096]{1,0:T(8,128)(2,1)}, bf16[576,4096]{1,0:T(8,128)(2,1)S(1)}, u32[]{:S(2)}, u32[]{:S(2)}) collective-permute-start(bf16[576,4096]{1,0:T(8,128)(2,1)} %copy-done.1), channel_id=1, source_target_pairs={{3,1},{1,3},{6,4},{4,6}} | collective-permute-start | bytes 14155784 | tf_op jit(solution)/shard_map/ppermute | solution.py:226
  824.3 121.0 %collective-permute-start.8 = (bf16[128,4096]{1,0:T(8,128)(2,1)S(1)}, bf16[128,4096]{1,0:T(8,128)(2,1)S(1)}, u32[]{:S(2)}, u32[]{:S(2)}) collective-permute-start(bf16[128,4096]{1,0:T(8,128)(2,1)S(1)} %get-tuple-element.11), channel_id=1, source_target_pairs={{3,1},{1,3},{6,4},{4,6}} | collective-permute-start | bytes 3145736 | tf_op jit(solution)/shard_map/ppermute | solution.py:226
  862.2 83.8 %collective-permute-start.7 = (bf16[64,4096]{1,0:T(8,128)(2,1)}, bf16[64,4096]{1,0:T(8,128)(2,1)}, u32[]{:S(2)}, u32[]{:S(2)}) collective-permute-start(bf16[64,4096]{1,0:T(8,128)(2,1)} %get-tuple-element.10), channel_id=1, source_target_pairs={{3,1},{1,3},{6,4},{4,6}} | collective-permute-start | bytes 1572872 | tf_op jit(solution)/shard_map/ppermute | solution.py:226

commit v3 on v2

--- a/solution.py
+++ b/solution.py
@@ -13,7 +13,7 @@
 LAG = 3
 VMEM_LIMIT = 32 * 1024 * 1024
 BOTH_ROWS = 768
-LAST_ROWS = (576, 128, 64)
+LAST_ROWS = (640, 96, 32)
 
 
 def _shard(dp, ep, slots, a, g, j):
@@ -122,12 +122,25 @@
         def picks(place_ref, me):
             return [lax.rem(place_ref[0, me * slots + j], n_exp) for j in range(slots)]
 
-        def early(place_ref, me, flip):
+        def early(pick, me, flip):
             e = me * 0
-            for j in range(slots):
-                for n in relayed[j]:
-                    e = jnp.where(me == n ^ flip, lax.rem(place_ref[0, n * slots + j], n_exp), e)
+            for _, n in to_x:
+                on = [j for j in range(slots) if n ^ 1 in relayed[j]]
+                here = [j for j in range(slots) if n in across[j]]
+                if on:
+                    first = pick(n ^ 1, on[0])
+                else:
+                    first = jnp.where(2 * sum(pick(n, j) for j in here) > len(here), 1, 0)
+                e = jnp.where(me == n ^ flip, first, e)
             return e
+
+        def scalars(place_ref):
+            return lambda n, j: lax.rem(place_ref[0, n * slots + j], n_exp)
+
+        def bits(place_ref):
+            lane = lax.broadcasted_iota(jnp.int32, place_ref.shape, 1)
+            mask = jnp.sum(jnp.left_shift(jnp.bitwise_and(place_ref[...], 1), lane))
+            return lambda n, j: jnp.bitwise_and(jnp.right_shift(mask, n * slots + j), 1)
 
         def call(kernel, out_shape, in_specs, scratch, size, aliases=None):
             return pl.pallas_call(
@@ -169,9 +182,9 @@
                     def _():
                         _one(rel.at[e[j]], [dest(out, j)], [True], buf, rs, ws)
 
-        def wants(place_ref, me, first):
-            e, a = picks(place_ref, me), early(place_ref, me, 1)
-            return [jnp.logical_and(_any(me, across[j]), (e[j] == a) == first) if across[j] else None
+        def wants(pick, me, first):
+            a = early(pick, me, 0)
+            return [jnp.logical_and(_any(me, across[j]), (pick(me, j) == a) == first) if across[j] else None
                     for j in range(slots)]
 
         def first_kernel(dest, place_ref, got, rel, _, out, buf, rs, ws):
@@ -179,7 +192,7 @@
 
             @pl.when(_any(me, sum(across, [])))
             def _():
-                _one(got, [dest(out, j) for j in range(slots)], wants(place_ref, me, True), buf, rs, ws)
+                _one(got, [dest(out, j) for j in range(slots)], wants(scalars(place_ref), me, True), buf, rs, ws)
 
             for j in range(slots):
                 if relayed[j]:
@@ -190,7 +203,7 @@
                         copy.wait()
 
         def last_kernel(dest, place_ref, got, _, out, ws):
-            want = wants(place_ref, where(), False)
+            want = wants(bits(place_ref), where(), False)
             for act in (lambda c: c.start(), lambda c: c.wait()):
                 for j in range(slots):
                     if want[j] is not None:
@@ -200,7 +213,7 @@
 
         def cut_kernel(place_ref, d, both, first, *rest):
             lasts, (buf, rs, ws) = rest[:-3], rest[-3:]
-            e = early(place_ref, where(), 3)
+            e = early(scalars(place_ref), where(), 2)
             tile = buf.shape[2]
             steps = []
             for x in range(n_exp):
@@ -252,7 +265,7 @@
         r = BOTH_ROWS
         for got in got_d[2:]:
             w2 = call(functools.partial(last_kernel, lambda o, j, r=r: rows_of(o, j, r)),
-                      shape(*w2.shape), [smem, vmem, hbm], [pltpu.SemaphoreType.DMA((slots,))],
+                      shape(*w2.shape), [vmem, vmem, hbm], [pltpu.SemaphoreType.DMA((slots,))],
                       3 * got.size * 2, {2: 0})(place, got, w2)
             r += got.shape[0]
         return w13[None], w2[None]

time: 984 us -> 983 us (level)
  no operation moved by 1% of the time
where the time goes in v3:
time: 983 us
  waiting for transfers between devices  785 us (80%)
  Pallas kernels  132 us (13%)
  starting transfers between devices  62.4 us (6%)
    ppermute x14, waiting for transfers between devices, permute(): return lax.ppermute(x, axes, pairs)  785 us
    pallas_call x1, Pallas kernels, hand_over(): call(own_kernel, (shape(slots, D, 2 * F), shape(slots, F, D)), [smem] + [...  67.5 us
    ppermute x14, starting transfers between devices, permute(): return lax.ppermute(x, axes, pairs)  62.4 us
    pallas_call x4, Pallas kernels, later(): call(functools.partial(kernel, dest), shape(*out.shape), [smem, hbm, rel_...  47.9 us
  transfers between devices with their start and end apart: 14, of which 4 were waited for; matrix products, arithmetic and copies ran while one was open for 0% of the time, Pallas kernels for 12%

profile of v3, /device:TPU:1, one launch (start us, length us, event | category | flops | bytes accessed | tf_op | source)
XLA Modules:
  0.0 982.6 jit_solution(18186104145625005448)
XLA Ops:
  0.6 3.9 collective-permute-start.2
  4.6 1.9 collective-permute-start
  7.2 14.8 %shard_map.62 = (bf16[2,768,4096]{2,1,0:T(8,128)(2,1)}, bf16[768,4096]{1,0:T(8,128)(2,1)S(1)}, bf16[640,4096]{1,0:T(8,128)(2,1)S(1)}, bf16[96,4096]{1,0:T(8,128)(2,1)S(1)}, bf16[32,4096]{1,0:T(8,128)(2,1)}) custom-call(s32[1,32]{1,0:T(1,128)S(1)} %copy-done, bf16[2,1536,4096]{2,1,0:T(8,128)(2,1)} %bitcast.6), custom_call_target="tpu_custom_call" | custom-call | bytes 50331648 | tf_op jit(solution)/shard_map/pallas_call | solution.py:247
  21.9 2.3 copy-done.1
  24.2 3.3 collective-permute-start.12
  27.6 1.9 collective-permute-start.10
  29.5 1.3 collective-permute-start.4
  30.8 716.4 %collective-permute-done.10.got = bf16[768,4096]{1,0:T(8,128)(2,1)S(1)} collective-permute-done((bf16[768,4096]{1,0:T(8,128)(2,1)S(1)}, bf16[768,4096]{1,0:T(8,128)(2,1)S(1)}, u32[]{:S(2)}, u32[]{:S(2)}) %collective-permute-start.10) | collective-permute-done | bytes 6291488 | tf_op jit(solution)/shard_map/ppermute | solution.py:239
  747.3 1.7 collective-permute-start.11
  749.0 1.3 collective-permute-start.5
  750.3 8.1 collective-permute-done.11.rel
  759.6 19.9 %collective-permute-start.3 = (bf16[2,4096,1536]{2,1,0:T(8,128)(2,1)}, bf16[2,4096,1536]{2,1,0:T(8,128)(2,1)}, u32[]{:S(2)}, u32[]{:S(2)}) collective-permute-start(bf16[2,4096,1536]{2,1,0:T(8,128)(2,1)} %collective-permute-done.2.got), channel_id=1, source_target_pairs={{1,0},{3,2}} | collective-permute-start | bytes 75497480 | tf_op jit(solution)/shard_map/ppermute | solution.py:239
  779.5 9.5 collective-permute-start.1
  789.0 6.3 collective-permute-start.13
  795.3 3.4 collective-permute-start.9
  798.6 25.7 %collective-permute-done.6.cd = bf16[2,1536,4096]{2,1,0:T(8,128)(2,1)} collective-permute-done((bf16[2,1536,4096]{2,1,0:T(8,128)(2,1)}, bf16[2,1536,4096]{2,1,0:T(8,128)(2,1)}, u32[]{:S(2)}, u32[]{:S(2)}) %collective-permute-start.6) | collective-permute-done | bytes 25165856 | tf_op jit(solution)/shard_map/ppermute | solution.py:239
  824.3 3.4 collective-permute-start.8
  827.7 34.5 %collective-permute-done.13.rel = bf16[2,768,4096]{2,1,0:T(8,128)(2,1)} collective-permute-done((bf16[2,768,4096]{2,1,0:T(8,128)(2,1)S(1)}, bf16[2,768,4096]{2,1,0:T(8,128)(2,1)}, u32[]{:S(2)}, u32[]{:S(2)}) %collective-permute-start.13) | collective-permute-done | bytes 12582944 | tf_op jit(solution)/shard_map/ppermute | solution.py:239
  862.2 3.4 collective-permute-start.7
  865.6 67.5 %shard_map.59 = (bf16[4,4096,3072]{2,1,0:T(8,128)(2,1)}, bf16[4,1536,4096]{2,1,0:T(8,128)(2,1)}) custom-call(s32[1,32]{1,0:T(1,128)S(1)} %copy-done, bf16[2,4096,1536]{2,1,0:T(8,128)(2,1)} %bitcast.14, bf16[2,4096,1536]{2,1,0:T(8,128)(2,1)} %bitcast.11, bf16[2,1536,4096]{2,1,0:T(8,128)(2,1)} %bitcast.8, bf16[2,4096,1536]{2,1,0:T(8,128)(2,1)} %copy-done.2, ...), custom_call_target="tpu_custom_call" | custom-call | bytes 150994944 | tf_op jit(solution)/shard_map/pallas_call | solution.py:252
  933.1 5.8 shard_map.63._
  938.9 5.9 shard_map.64._
  946.3 18.1 %shard_map.60._ = bf16[4,4096,3072]{2,1,0:T(8,128)(2,1)} custom-call(s32[1,32]{1,0:T(1,128)S(1)} %copy-done, bf16[2,4096,1536]{2,1,0:T(8,128)(2,1)} %collective-permute-done.2.got, bf16[2,4096,1536]{2,1,0:T(8,128)(2,1)} %collective-permute-done.3.rel, bf16[4,4096,3072]{2,1,0:T(8,128)(2,1)} %get-tuple-element.9._), custom_call_target="tpu_custom_call", output_to_operand_aliasing={{}: (3, {})} | custom-call | bytes 75497472 | tf_op jit(solution)/shard_map/pallas_call | solution.py:257
  964.5 18.1 %shard_map.61 = bf16[4,4096,3072]{2,1,0:T(8,128)(2,1)} custom-call(s32[1,32]{1,0:T(1,128)S(1)} %copy-done, bf16[2,4096,1536]{2,1,0:T(8,128)(2,1)} %collective-permute-done.got, bf16[2,4096,1536]{2,1,0:T(8,128)(2,1)} %collective-permute-done.1.rel, bf16[4,4096,3072]{2,1,0:T(8,128)(2,1)} %shard_map.60._), custom_call_target="tpu_custom_call", output_to_operand_aliasing={{}: (3, {})} | custom-call | bytes 75497472 | tf_op jit(solution)/shard_map/pallas_call | solution.py:257
  (19 shorter events, 3.5 us)
Async XLA Ops:
  0.6 759.0 %collective-permute-start.2 = (bf16[2,4096,1536]{2,1,0:T(8,128)(2,1)}, bf16[2,4096,1536]{2,1,0:T(8,128)(2,1)}, u32[]{:S(2)}, u32[]{:S(2)}) collective-permute-start(bf16[2,4096,1536]{2,1,0:T(8,128)(2,1)} %bitcast.12), channel_id=1, source_target_pairs={{3,1},{1,3},{6,4},{4,6}} | collective-permute-start | bytes 75497480 | tf_op jit(solution)/shard_map/ppermute | solution.py:239
  4.6 774.9 %collective-permute-start = (bf16[2,4096,1536]{2,1,0:T(8,128)(2,1)}, bf16[2,4096,1536]{2,1,0:T(8,128)(2,1)}, u32[]{:S(2)}, u32[]{:S(2)}) collective-permute-start(bf16[2,4096,1536]{2,1,0:T(8,128)(2,1)} %bitcast.9), channel_id=1, source_target_pairs={{3,1},{1,3},{6,4},{4,6}} | collective-permute-start | bytes 75497480 | tf_op jit(solution)/shard_map/ppermute | solution.py:239
  6.5 0.7 copy-start
  21.9 2.3 copy-start.1
  24.2 724.7 %collective-permute-start.12 = (bf16[2,768,4096]{2,1,0:T(8,128)(2,1)}, bf16[2,768,4096]{2,1,0:T(8,128)(2,1)S(1)}, u32[]{:S(2)}, u32[]{:S(2)}) collective-permute-start(bf16[2,768,4096]{2,1,0:T(8,128)(2,1)} %get-tuple-element.14), channel_id=1, source_target_pairs={{3,1},{1,3},{6,4},{4,6}} | collective-permute-start | bytes 37748744 | tf_op jit(solution)/shard_map/ppermute | solution.py:239
  27.6 719.7 %collective-permute-start.10 = (bf16[768,4096]{1,0:T(8,128)(2,1)S(1)}, bf16[768,4096]{1,0:T(8,128)(2,1)S(1)}, u32[]{:S(2)}, u32[]{:S(2)}) collective-permute-start(bf16[768,4096]{1,0:T(8,128)(2,1)S(1)} %get-tuple-element.13), channel_id=1, source_target_pairs={{3,1},{1,3},{6,4},{4,6}} | collective-permute-start | bytes 18874376 | tf_op jit(solution)/shard_map/ppermute | solution.py:239
  29.5 759.5 %collective-permute-start.4 = (bf16[2,4096,1536]{2,1,0:T(8,128)(2,1)}, bf16[2,4096,1536]{2,1,0:T(8,128)(2,1)S(1)}, u32[]{:S(2)}, u32[]{:S(2)}) collective-permute-start(bf16[2,4096,1536]{2,1,0:T(8,128)(2,1)} %bitcast.13), channel_id=1, source_target_pairs={{0,1},{2,3}} | collective-permute-start | bytes 75497480 | tf_op jit(solution)/shard_map/ppermute | solution.py:239
  747.3 11.1 %collective-permute-start.11 = (bf16[768,4096]{1,0:T(8,128)(2,1)S(1)}, bf16[768,4096]{1,0:T(8,128)(2,1)S(1)}, u32[]{:S(2)}, u32[]{:S(2)}) collective-permute-start(bf16[768,4096]{1,0:T(8,128)(2,1)S(1)} %collective-permute-done.10.got), channel_id=1, source_target_pairs={{1,0},{3,2}} | collective-permute-start | bytes 18874376 | tf_op jit(solution)/shard_map/ppermute | solution.py:239
  749.0 46.3 %collective-permute-start.5 = (bf16[2,4096,1536]{2,1,0:T(8,128)(2,1)}, bf16[2,4096,1536]{2,1,0:T(8,128)(2,1)}, u32[]{:S(2)}, u32[]{:S(2)}) collective-permute-start(bf16[2,4096,1536]{2,1,0:T(8,128)(2,1)} %bitcast.10), channel_id=1, source_target_pairs={{0,1},{2,3}} | collective-permute-start | bytes 75497480 | tf_op jit(solution)/shard_map/ppermute | solution.py:239
  758.3 66.0 %collective-permute-start.6 = (bf16[2,1536,4096]{2,1,0:T(8,128)(2,1)}, bf16[2,1536,4096]{2,1,0:T(8,128)(2,1)}, u32[]{:S(2)}, u32[]{:S(2)}) collective-permute-start(bf16[2,1536,4096]{2,1,0:T(8,128)(2,1)} %bitcast.7), channel_id=1, source_target_pairs={{0,1},{2,3}} | collective-permute-start | bytes 75497480 | tf_op jit(solution)/shard_map/ppermute | solution.py:239
  759.6 186.7 %collective-permute-start.3 = (bf16[2,4096,1536]{2,1,0:T(8,128)(2,1)}, bf16[2,4096,1536]{2,1,0:T(8,128)(2,1)}, u32[]{:S(2)}, u32[]{:S(2)}) collective-permute-start(bf16[2,4096,1536]{2,1,0:T(8,128)(2,1)} %collective-permute-done.2.got), channel_id=1, source_target_pairs={{1,0},{3,2}} | collective-permute-start | bytes 75497480 | tf_op jit(solution)/shard_map/ppermute | solution.py:239
  779.5 185.0 %collective-permute-start.1 = (bf16[2,4096,1536]{2,1,0:T(8,128)(2,1)}, bf16[2,4096,1536]{2,1,0:T(8,128)(2,1)}, u32[]{:S(2)}, u32[]{:S(2)}) collective-permute-start(bf16[2,4096,1536]{2,1,0:T(8,128)(2,1)} %collective-permute-done.got), channel_id=1, source_target_pairs={{1,0},{3,2}} | collective-permute-start | bytes 75497480 | tf_op jit(solution)/shard_map/ppermute | solution.py:239
  789.0 73.2 %copy-start.2 = (bf16[2,4096,1536]{2,1,0:T(8,128)(2,1)}, bf16[2,4096,1536]{2,1,0:T(8,128)(2,1)S(1)}, u32[]{:S(2)}) copy-start(bf16[2,4096,1536]{2,1,0:T(8,128)(2,1)S(1)} %collective-permute-done.4.cg) | copy-start | bytes 75497472
  789.0 73.2 %collective-permute-start.13 = (bf16[2,768,4096]{2,1,0:T(8,128)(2,1)S(1)}, bf16[2,768,4096]{2,1,0:T(8,128)(2,1)}, u32[]{:S(2)}, u32[]{:S(2)}) collective-permute-start(bf16[2,768,4096]{2,1,0:T(8,128)(2,1)S(1)} %collective-permute-done.12.got), channel_id=1, source_target_pairs={{1,0},{3,2}} | collective-permute-start | bytes 37748744 | tf_op jit(solution)/shard_map/ppermute | solution.py:239
  795.3 149.5 %collective-permute-start.9 = (bf16[640,4096]{1,0:T(8,128)(2,1)}, bf16[640,4096]{1,0:T(8,128)(2,1)S(1)}, u32[]{:S(2)}, u32[]{:S(2)}) collective-permute-start(bf16[640,4096]{1,0:T(8,128)(2,1)} %copy-done.1), channel_id=1, source_target_pairs={{3,1},{1,3},{6,4},{4,6}} | collective-permute-start | bytes 15728648 | tf_op jit(solution)/shard_map/ppermute | solution.py:239
  824.3 120.6 %collective-permute-start.8 = (bf16[96,4096]{1,0:T(8,128)(2,1)S(1)}, bf16[96,4096]{1,0:T(8,128)(2,1)S(1)}, u32[]{:S(2)}, u32[]{:S(2)}) collective-permute-start(bf16[96,4096]{1,0:T(8,128)(2,1)S(1)} %get-tuple-element.11), channel_id=1, source_target_pairs={{3,1},{1,3},{6,4},{4,6}} | collective-permute-start | bytes 2359304 | tf_op jit(solution)/shard_map/ppermute | solution.py:239
  862.2 82.9 %collective-permute-start.7 = (bf16[32,4096]{1,0:T(8,128)(2,1)}, bf16[32,4096]{1,0:T(8,128)(2,1)}, u32[]{:S(2)}, u32[]{:S(2)}) collective-permute-start(bf16[32,4096]{1,0:T(8,128)(2,1)} %get-tuple-element.10), channel_id=1, source_target_pairs={{3,1},{1,3},{6,4},{4,6}} | collective-permute-start | bytes 786440 | tf_op jit(solution)/shard_map/ppermute | solution.py:239

commit v4 on v3

v4 whole, which is shorter than its diff:
```python
import functools

import jax
import jax.numpy as jnp
from jax import lax
from jax.experimental import pallas as pl
from jax.experimental.pallas import tpu as pltpu
from jax.sharding import PartitionSpec as P


VMEM_LIMIT = 40 * 1024 * 1024
BOTH_ROWS = 768
LAST_ROWS = (672, 80, 16)
N_PIECES = 2 + len(LAST_ROWS)


def _shard(dp, ep, slots, a, g, j):
    return (2 * a - g) % ep if j < ((a + 1) * slots) // dp else (g + j + 1) % ep


def _devices(dp, ep, slots, flip):
    return [[a * ep + g for a in range(dp) for g in range(ep) if _shard(dp, ep, slots, a, g, j) == g ^ flip]
            for j in range(slots)]


def _any(me, devices):
    hit = me < 0
    for n in sorted(set(devices)):
        hit = jnp.logical_or(hit, me == n)
    return hit


def _place(src, buf, sem, dests, views, who, wsem):
    read = pltpu.make_async_copy(src, buf, sem)
    read.start()
    read.wait()
    for act in (lambda c: c.start(), lambda c: c.wait()):
        for j, dest in enumerate(dests):
            if who[j] is not None:
                @pl.when(who[j])
                def _():
                    act(pltpu.make_async_copy(views[j], dest, wsem.at[j]))


def solution(mesh):
    dp = mesh.shape["dp"]
    ep = mesh.shape["ep"]
    axes = ("dp", "ep")
    hbm = pl.BlockSpec(memory_space=pltpu.HBM)
    vmem = pl.BlockSpec(memory_space=pltpu.VMEM)
    smem = pl.BlockSpec(memory_space=pltpu.SMEM)

    def hand_over(w_gate, w_up, w_down, place):
        wg, wu, wd = w_gate[0], w_up[0], w_down[0]
        n_exp, D, F = wg.shape
        slots = place.shape[1] // (dp * ep)
        own, across, beside, relayed = (_devices(dp, ep, slots, f) for f in (0, 2, 1, 3))
        to_x = [(n ^ 2, n) for n in sorted(set(sum(across, [])) | {m ^ 1 for m in sum(relayed, [])})]
        to_core = [(n ^ 1, n) for n in sorted(set(sum(beside, [])))]
        to_relay = [(n ^ 1, n) for n in sorted(set(sum(relayed, [])))]

        def buffer(*dims):
            return [pltpu.VMEM(dims, jnp.bfloat16), pltpu.SemaphoreType.DMA, pltpu.SemaphoreType.DMA((slots,))]

        def where():
            return lax.axis_index("dp") * ep + lax.axis_index("ep")

        def half(out, j, k):
            return out.at[j, :, pl.ds(k * F, F)]

        def rows_of(out, j, first, n):
            return out.at[j, pl.ds(first, n)]

        def at(me, devices):
            return [_any(me, d) if d else None for d in devices]

        def picks(place_ref, me):
            return [lax.rem(place_ref[0, me * slots + j], n_exp) for j in range(slots)]

        def early(pick, me, flip):
            e = me * 0
            for _, n in to_x:
                on = [j for j in range(slots) if n ^ 1 in relayed[j]]
                here = [j for j in range(slots) if n in across[j]]
                if on:
                    first = pick(n ^ 1, on[0])
                else:
                    first = jnp.where(2 * sum(pick(n, j) for j in here) > len(here), 1, 0)
                e = jnp.where(me == n ^ flip, first, e)
            return e

        def scalars(place_ref):
            return lambda n, j: lax.rem(place_ref[0, n * slots + j], n_exp)

        def bits(place_ref):
            lane = lax.broadcasted_iota(jnp.int32, place_ref.shape, 1)
            mask = jnp.sum(jnp.left_shift(jnp.bitwise_and(place_ref[...], 1), lane))
            return lambda n, j: jnp.bitwise_and(jnp.right_shift(mask, n * slots + j), 1)

        def call(kernel, out_shape, in_specs, scratch, size, aliases=None):
            return pl.pallas_call(
                kernel, out_shape=out_shape, in_specs=in_specs,
                out_specs=jax.tree.map(lambda _: hbm, out_shape), scratch_shapes=scratch,
                input_output_aliases=aliases or {},
                compiler_params=pltpu.CompilerParams(vmem_limit_bytes=VMEM_LIMIT),
                cost_estimate=pl.CostEstimate(flops=0, bytes_accessed=size, transcendentals=0))

        def own_kernel(place_ref, g, u, d, cg, cu, cd, o13, o2, buf_f, sf, wf, buf_d, sd, wd_):
            me = where()
            e = picks(place_ref, me)
            n = buf_d.shape[1]
            for who, blocks in ((own, (g, u, d)), (beside, (cg, cu, cd))):
                @pl.when(_any(me, sum(who, [])))
                def _():
                    for k in range(2):
                        _place(blocks[k], buf_f, sf, [half(o13, j, k) for j in range(slots)],
                               [buf_f.at[e[j]] for j in range(slots)], at(me, who), wf)
                    for r in range(0, F, n):
                        _place(blocks[2].at[:, pl.ds(r, n)], buf_d, sd, [rows_of(o2, j, r, n) for j in range(slots)],
                               [buf_d.at[e[j]] for j in range(slots)], at(me, who), wd_)

        def both_kernel(dest, place_ref, got, rel, _, out, buf, sem, ws):
            me = where()
            e = picks(place_ref, me)
            for who, src in ((across, got), (relayed, rel)):
                @pl.when(_any(me, sum(who, [])))
                def _():
                    _place(src, buf, sem, [dest(out, j) for j in range(slots)],
                           [buf.at[e[j]] for j in range(slots)], at(me, who), ws)

        def wants(pick, me, first):
            a = early(pick, me, 0)
            return [jnp.logical_and(_any(me, across[j]), (pick(me, j) == a) == first) if across[j] else None
                    for j in range(slots)]

        def first_kernel(dest, place_ref, got, rel, _, out, buf, sem, ws):
            me = where()

            @pl.when(_any(me, sum(across, [])))
            def _():
                _place(got, buf, sem, [dest(out, j) for j in range(slots)], [buf] * slots,
                       wants(scalars(place_ref), me, True), ws)

            for j in range(slots):
                if relayed[j]:
                    @pl.when(_any(me, relayed[j]))
                    def _():
                        copy = pltpu.make_async_copy(rel, dest(out, j), sem)
                        copy.start()
                        copy.wait()

        def last_kernel(dest, place_ref, got, _, out, ws):
            want = wants(bits(place_ref), where(), False)
            for act in (lambda c: c.start(), lambda c: c.wait()):
                for j in range(slots):
                    if want[j] is not None:
                        @pl.when(want[j])
                        def _():
                            act(pltpu.make_async_copy(got, dest(out, j), ws.at[j]))

        def cut_kernel(place_ref, d, both, *rest):
            pieces, (buf, sem, ws) = rest[:-3], rest[-3:]
            e = early(scalars(place_ref), where(), 2)
            read = pltpu.make_async_copy(d, buf, sem)
            read.start()
            read.wait()
            writes = [pltpu.make_async_copy(buf.at[:, pl.ds(0, BOTH_ROWS)], both, ws.at[0])]
            r = BOTH_ROWS
            for i, o in enumerate(pieces):
                x = e if i == 0 else 1 - e
                writes.append(pltpu.make_async_copy(buf.at[x, pl.ds(r, o.shape[0])], o, ws.at[i + 1]))
                r = BOTH_ROWS if i == 0 else r + o.shape[0]
            for w in writes:
                w.start()
            for w in writes:
                w.wait()

        def permute(x, pairs):
            return lax.ppermute(x, axes, pairs)

        def shape(*dims):
            return jax.ShapeDtypeStruct(dims, jnp.bfloat16)

        block = wg.size * wg.dtype.itemsize
        got_g = permute(wg, to_x)
        got_u = permute(wu, to_x)
        cuts = call(cut_kernel,
                    [shape(n_exp, BOTH_ROWS, D), shape(F - BOTH_ROWS, D)] + [shape(n, D) for n in LAST_ROWS],
                    [smem, hbm], [pltpu.VMEM(wd.shape, jnp.bfloat16), pltpu.SemaphoreType.DMA,
                                  pltpu.SemaphoreType.DMA((N_PIECES,))], 2 * block)(place, wd)
        got_d = [permute(c, to_x) for c in cuts]
        side = [permute(w, to_core) for w in (wg, wu, wd)]
        w13, w2 = call(own_kernel, (shape(slots, D, 2 * F), shape(slots, F, D)),
                       [smem] + [hbm] * 6, buffer(*wg.shape) + buffer(n_exp, F // 2, D),
                       6 * block)(place, wg, wu, wd, *side)

        def later(kernel, dest, got, out, rel_in=hbm):
            rel = permute(got, to_relay)
            return call(functools.partial(kernel, dest), shape(*out.shape), [smem, hbm, rel_in, hbm],
                        buffer(*got.shape), 3 * got.size * 2, {3: 0})(place, got, rel, out)

        w13 = later(both_kernel, lambda o, j: half(o, j, 0), got_g, w13)
        w13 = later(both_kernel, lambda o, j: half(o, j, 1), got_u, w13)
        w2 = later(both_kernel, lambda o, j: rows_of(o, j, 0, BOTH_ROWS), got_d[0], w2)
        w2 = later(first_kernel, lambda o, j: rows_of(o, j, BOTH_ROWS, F - BOTH_ROWS), got_d[1], w2,
                   vmem)
        r = BOTH_ROWS
        for got in got_d[2:]:
            n = got.shape[0]
            w2 = call(functools.partial(last_kernel, lambda o, j, r=r, n=n: rows_of(o, j, r, n)),
                      shape(*w2.shape), [vmem, vmem, hbm], [pltpu.SemaphoreType.DMA((slots,))],
                      3 * got.size * 2, {2: 0})(place, got, w2)
            r += n
        return w13[None], w2[None]

    spec_in = P(None, "ep", None, None)
    spec_out = P(None, ("dp", "ep"), None, None)
    return jax.shard_map(hand_over, mesh=mesh,
                         in_specs=(spec_in, spec_in, spec_in, P(None, None)),
                         out_specs=(spec_out, spec_out), check_vma=False)
```

time: 983 us -> 1000 us (1.017)
  local copies, waits for them, and re-layouts: 2.93 us -> 19.5 us
  Pallas kernels: 132 us -> 146 us
  waiting for transfers between devices: 785 us -> 773 us
    unnamed x6 -> x18, local copies, waits for them, and re-layouts: 2.93 us -> 19.5 us
    pallas_call x1, Pallas kernels: 67.5 us -> 81.5 us  [hand_over(): call(own_kernel, (shape(slots, D, 2 * F), shape(slots, F, D)), [smem] + [...]
    ppermute x14, waiting for transfers between devices: 785 us -> 773 us  [permute(): return lax.ppermute(x, axes, pairs)]
  transfers between devices with their start and end apart: 14 -> 14, of which waited for: 4 -> 4; matrix products, arithmetic and copies ran while one was open for 0% -> 0% of each run, Pallas kernels for 12% -> 13%
where the time goes in v4:
time: 1000 us
  waiting for transfers between devices  773 us (77%)
  Pallas kernels  146 us (15%)
  starting transfers between devices  62.1 us (6%)
  local copies, waits for them, and re-layouts  19.5 us (2%)
    ppermute x14, waiting for transfers between devices, permute(): return lax.ppermute(x, axes, pairs)  773 us
    pallas_call x1, Pallas kernels, hand_over(): call(own_kernel, (shape(slots, D, 2 * F), shape(slots, F, D)), [smem] + [...  81.5 us
    ppermute x14, starting transfers between devices, permute(): return lax.ppermute(x, axes, pairs)  62.1 us
    pallas_call x4, Pallas kernels, later(): call(functools.partial(kernel, dest), shape(*out.shape), [smem, hbm, rel_...  47.4 us
  transfers between devices with their start and end apart: 14, of which 4 were waited for; matrix products, arithmetic and copies ran while one was open for 0% of the time, Pallas kernels for 13%

profile of v4, /device:TPU:1, one launch (start us, length us, event | category | flops | bytes accessed | tf_op | source)
XLA Modules:
  0.0 1001.7 jit_solution(16633056462989208025)
XLA Ops:
  0.6 3.9 collective-permute-start.2
  4.6 1.9 collective-permute-start
  7.2 15.4 %shard_map.62 = (bf16[2,768,4096]{2,1,0:T(8,128)(2,1)}, bf16[768,4096]{1,0:T(8,128)(2,1)S(1)}, bf16[672,4096]{1,0:T(8,128)(2,1)}, bf16[80,4096]{1,0:T(8,128)(2,1)}, bf16[16,4096]{1,0:T(8,128)(2,1)S(1)}) custom-call(s32[1,32]{1,0:T(1,128)S(1)} %copy-done.3, bf16[2,1536,4096]{2,1,0:T(8,128)(2,1)} %bitcast.8), custom_call_target="tpu_custom_call" | custom-call | bytes 50331648 | tf_op jit(solution)/shard_map/pallas_call | solution.py:187
  23.2 3.3 collective-permute-start.12
  26.6 1.9 collective-permute-start.10
  29.8 717.4 %collective-permute-done.10.got = bf16[768,4096]{1,0:T(8,128)(2,1)S(1)} collective-permute-done((bf16[768,4096]{1,0:T(8,128)(2,1)S(1)}, bf16[768,4096]{1,0:T(8,128)(2,1)S(1)}, u32[]{:S(2)}, u32[]{:S(2)}) %collective-permute-start.10) | collective-permute-done | bytes 6291488 | tf_op jit(solution)/shard_map/ppermute | solution.py:179
  750.3 8.1 collective-permute-done.11.rel
  758.3 2.7 copy-done.1
  762.3 19.6 %collective-permute-start.3 = (bf16[2,4096,1536]{2,1,0:T(8,128)(2,1)}, bf16[2,4096,1536]{2,1,0:T(8,128)(2,1)}, u32[]{:S(2)}, u32[]{:S(2)}) collective-permute-start(bf16[2,4096,1536]{2,1,0:T(8,128)(2,1)} %collective-permute-done.2.got), channel_id=1, source_target_pairs={{1,0},{3,2}} | collective-permute-start | bytes 75497480 | tf_op jit(solution)/shard_map/ppermute | solution.py:179
  781.8 9.5 collective-permute-start.1
  791.4 5.9 collective-permute-start.13
  797.2 4.5 copy-done
  801.7 8.3 copy-done.5
  810.0 3.3 collective-permute-start.9
  813.4 11.0 %collective-permute-done.6.cd = bf16[2,1536,4096]{2,1,0:T(8,128)(2,1)} collective-permute-done((bf16[2,1536,4096]{2,1,0:T(8,128)(2,1)}, bf16[2,1536,4096]{2,1,0:T(8,128)(2,1)}, u32[]{:S(2)}, u32[]{:S(2)}) %collective-permute-start.6) | collective-permute-done | bytes 25165856 | tf_op jit(solution)/shard_map/ppermute | solution.py:179
  824.3 3.4 collective-permute-start.8
  827.7 36.9 %collective-permute-done.13.rel = bf16[2,768,4096]{2,1,0:T(8,128)(2,1)} collective-permute-done((bf16[2,768,4096]{2,1,0:T(8,128)(2,1)S(1)}, bf16[2,768,4096]{2,1,0:T(8,128)(2,1)}, u32[]{:S(2)}, u32[]{:S(2)}) %collective-permute-start.13) | collective-permute-done | bytes 12582944 | tf_op jit(solution)/shard_map/ppermute | solution.py:179
  864.6 3.7 collective-permute-start.7
  868.4 81.5 %shard_map.59 = (bf16[4,4096,3072]{2,1,0:T(8,128)(2,1)}, bf16[4,1536,4096]{2,1,0:T(8,128)(2,1)}) custom-call(s32[1,32]{1,0:T(1,128)S(1)} %copy-done.3, bf16[2,4096,1536]{2,1,0:T(8,128)(2,1)} %bitcast.16, bf16[2,4096,1536]{2,1,0:T(8,128)(2,1)} %bitcast.13, bf16[2,1536,4096]{2,1,0:T(8,128)(2,1)} %bitcast.10, bf16[2,4096,1536]{2,1,0:T(8,128)(2,1)} %collective-permute-done.4.cg, ...), custom_call_target="tpu_custom_call" | custom-call | bytes 150994944 | tf_op jit(solution)/shard_map/pallas_call | solution.py:193
  949.9 6.2 shard_map.63._
  956.1 2.8 copy-done.2
  958.9 5.8 shard_map.64._
  966.3 17.7 %shard_map.60._ = bf16[4,4096,3072]{2,1,0:T(8,128)(2,1)} custom-call(s32[1,32]{1,0:T(1,128)S(1)} %copy-done.3, bf16[2,4096,1536]{2,1,0:T(8,128)(2,1)} %collective-permute-done.2.got, bf16[2,4096,1536]{2,1,0:T(8,128)(2,1)} %collective-permute-done.3.rel, bf16[4,4096,3072]{2,1,0:T(8,128)(2,1)} %get-tuple-element.9._), custom_call_target="tpu_custom_call", output_to_operand_aliasing={{}: (3, {})} | custom-call | bytes 75497472 | tf_op jit(solution)/shard_map/pallas_call | solution.py:199
  984.0 17.7 %shard_map.61 = bf16[4,4096,3072]{2,1,0:T(8,128)(2,1)} custom-call(s32[1,32]{1,0:T(1,128)S(1)} %copy-done.3, bf16[2,4096,1536]{2,1,0:T(8,128)(2,1)} %collective-permute-done.got, bf16[2,4096,1536]{2,1,0:T(8,128)(2,1)} %collective-permute-done.1.rel, bf16[4,4096,3072]{2,1,0:T(8,128)(2,1)} %shard_map.60._), custom_call_target="tpu_custom_call", output_to_operand_aliasing={{}: (3, {})} | custom-call | bytes 75497472 | tf_op jit(solution)/shard_map/pallas_call | solution.py:199
  (32 shorter events, 8.3 us)
Async XLA Ops:
  0.6 761.6 %collective-permute-start.2 = (bf16[2,4096,1536]{2,1,0:T(8,128)(2,1)}, bf16[2,4096,1536]{2,1,0:T(8,128)(2,1)}, u32[]{:S(2)}, u32[]{:S(2)}) collective-permute-start(bf16[2,4096,1536]{2,1,0:T(8,128)(2,1)} %bitcast.14), channel_id=1, source_target_pairs={{3,1},{1,3},{6,4},{4,6}} | collective-permute-start | bytes 75497480 | tf_op jit(solution)/shard_map/ppermute | solution.py:179
  4.6 777.3 %collective-permute-start = (bf16[2,4096,1536]{2,1,0:T(8,128)(2,1)}, bf16[2,4096,1536]{2,1,0:T(8,128)(2,1)}, u32[]{:S(2)}, u32[]{:S(2)}) collective-permute-start(bf16[2,4096,1536]{2,1,0:T(8,128)(2,1)} %bitcast.11), channel_id=1, source_target_pairs={{3,1},{1,3},{6,4},{4,6}} | collective-permute-start | bytes 75497480 | tf_op jit(solution)/shard_map/ppermute | solution.py:179
  6.5 0.7 copy-start.3
  22.6 0.6 copy-start.4
  23.2 725.7 %collective-permute-start.12 = (bf16[2,768,4096]{2,1,0:T(8,128)(2,1)}, bf16[2,768,4096]{2,1,0:T(8,128)(2,1)S(1)}, u32[]{:S(2)}, u32[]{:S(2)}) collective-permute-start(bf16[2,768,4096]{2,1,0:T(8,128)(2,1)} %get-tuple-element.14), channel_id=1, source_target_pairs={{3,1},{1,3},{6,4},{4,6}} | collective-permute-start | bytes 37748744 | tf_op jit(solution)/shard_map/ppermute | solution.py:179
  26.6 720.7 %collective-permute-start.10 = (bf16[768,4096]{1,0:T(8,128)(2,1)S(1)}, bf16[768,4096]{1,0:T(8,128)(2,1)S(1)}, u32[]{:S(2)}, u32[]{:S(2)}) collective-permute-start(bf16[768,4096]{1,0:T(8,128)(2,1)S(1)} %get-tuple-element.13), channel_id=1, source_target_pairs={{3,1},{1,3},{6,4},{4,6}} | collective-permute-start | bytes 18874376 | tf_op jit(solution)/shard_map/ppermute | solution.py:179
  28.5 762.8 %collective-permute-start.4 = (bf16[2,4096,1536]{2,1,0:T(8,128)(2,1)}, bf16[2,4096,1536]{2,1,0:T(8,128)(2,1)}, u32[]{:S(2)}, u32[]{:S(2)}) collective-permute-start(bf16[2,4096,1536]{2,1,0:T(8,128)(2,1)} %bitcast.15), channel_id=1, source_target_pairs={{0,1},{2,3}} | collective-permute-start | bytes 75497480 | tf_op jit(solution)/shard_map/ppermute | solution.py:179
  747.3 11.1 %collective-permute-start.11 = (bf16[768,4096]{1,0:T(8,128)(2,1)S(1)}, bf16[768,4096]{1,0:T(8,128)(2,1)S(1)}, u32[]{:S(2)}, u32[]{:S(2)}) collective-permute-start(bf16[768,4096]{1,0:T(8,128)(2,1)S(1)} %collective-permute-done.10.got), channel_id=1, source_target_pairs={{1,0},{3,2}} | collective-permute-start | bytes 18874376 | tf_op jit(solution)/shard_map/ppermute | solution.py:179
  749.0 52.7 %collective-permute-start.5 = (bf16[2,4096,1536]{2,1,0:T(8,128)(2,1)}, bf16[2,4096,1536]{2,1,0:T(8,128)(2,1)S(1)}, u32[]{:S(2)}, u32[]{:S(2)}) collective-permute-start(bf16[2,4096,1536]{2,1,0:T(8,128)(2,1)} %bitcast.12), channel_id=1, source_target_pairs={{0,1},{2,3}} | collective-permute-start | bytes 75497480 | tf_op jit(solution)/shard_map/ppermute | solution.py:179
  758.3 2.7 copy-start.1
  761.0 63.4 %collective-permute-start.6 = (bf16[2,1536,4096]{2,1,0:T(8,128)(2,1)}, bf16[2,1536,4096]{2,1,0:T(8,128)(2,1)}, u32[]{:S(2)}, u32[]{:S(2)}) collective-permute-start(bf16[2,1536,4096]{2,1,0:T(8,128)(2,1)} %bitcast.9), channel_id=1, source_target_pairs={{0,1},{2,3}} | collective-permute-start | bytes 75497480 | tf_op jit(solution)/shard_map/ppermute | solution.py:179
  762.3 204.0 %collective-permute-start.3 = (bf16[2,4096,1536]{2,1,0:T(8,128)(2,1)}, bf16[2,4096,1536]{2,1,0:T(8,128)(2,1)}, u32[]{:S(2)}, u32[]{:S(2)}) collective-permute-start(bf16[2,4096,1536]{2,1,0:T(8,128)(2,1)} %collective-permute-done.2.got), channel_id=1, source_target_pairs={{1,0},{3,2}} | collective-permute-start | bytes 75497480 | tf_op jit(solution)/shard_map/ppermute | solution.py:179
  781.8 202.1 %collective-permute-start.1 = (bf16[2,4096,1536]{2,1,0:T(8,128)(2,1)}, bf16[2,4096,1536]{2,1,0:T(8,128)(2,1)}, u32[]{:S(2)}, u32[]{:S(2)}) collective-permute-start(bf16[2,4096,1536]{2,1,0:T(8,128)(2,1)} %collective-permute-done.got), channel_id=1, source_target_pairs={{1,0},{3,2}} | collective-permute-start | bytes 75497480 | tf_op jit(solution)/shard_map/ppermute | solution.py:179
  791.4 73.2 %collective-permute-start.13 = (bf16[2,768,4096]{2,1,0:T(8,128)(2,1)S(1)}, bf16[2,768,4096]{2,1,0:T(8,128)(2,1)}, u32[]{:S(2)}, u32[]{:S(2)}) collective-permute-start(bf16[2,768,4096]{2,1,0:T(8,128)(2,1)S(1)} %collective-permute-done.12.got), channel_id=1, source_target_pairs={{1,0},{3,2}} | collective-permute-start | bytes 37748744 | tf_op jit(solution)/shard_map/ppermute | solution.py:179
  797.2 4.5 copy-start
  801.7 8.3 copy-start.5
  810.0 154.7 %collective-permute-start.9 = (bf16[672,4096]{1,0:T(8,128)(2,1)}, bf16[672,4096]{1,0:T(8,128)(2,1)S(1)}, u32[]{:S(2)}, u32[]{:S(2)}) collective-permute-start(bf16[672,4096]{1,0:T(8,128)(2,1)} %get-tuple-element.12), channel_id=1, source_target_pairs={{3,1},{1,3},{6,4},{4,6}} | collective-permute-start | bytes 16515080 | tf_op jit(solution)/shard_map/ppermute | solution.py:179
  824.3 140.6 %collective-permute-start.8 = (bf16[80,4096]{1,0:T(8,128)(2,1)}, bf16[80,4096]{1,0:T(8,128)(2,1)S(1)}, u32[]{:S(2)}, u32[]{:S(2)}) collective-permute-start(bf16[80,4096]{1,0:T(8,128)(2,1)} %get-tuple-element.11), channel_id=1, source_target_pairs={{3,1},{1,3},{6,4},{4,6}} | collective-permute-start | bytes 1966088 | tf_op jit(solution)/shard_map/ppermute | solution.py:179
  864.6 85.3 %slice-start = ((s8[12582912]{0:T(1024)(128)(4,1)}), s8[4194304]{0:T(1024)(128)(4,1)S(1)}, s32[]{:S(2)}) async-start(s8[12582912]{0:T(1024)(128)(4,1)} %bitcast.5), calls=%async_computation | async-start | bytes 8388608
  864.6 85.3 %slice-start.1 = ((s8[12582912]{0:T(1024)(128)(4,1)}), s8[4194304]{0:T(1024)(128)(4,1)S(1)}, s32[]{:S(2)}) async-start(s8[12582912]{0:T(1024)(128)(4,1)} %bitcast.5), calls=%async_computation.1 | async-start | bytes 8388608
  864.6 85.3 %slice-start.2 = ((s8[12582912]{0:T(1024)(128)(4,1)}), s8[4194304]{0:T(1024)(128)(4,1)S(1)}, s32[]{:S(2)}) async-start(s8[12582912]{0:T(1024)(128)(4,1)} %bitcast.5), calls=%async_computation.2 | async-start | bytes 8388608
  864.6 100.5 %collective-permute-start.7 = (bf16[16,4096]{1,0:T(8,128)(2,1)}, bf16[16,4096]{1,0:T(8,128)(2,1)}, u32[]{:S(2)}, u32[]{:S(2)}) collective-permute-start(bf16[16,4096]{1,0:T(8,128)(2,1)} %copy-done.4), channel_id=1, source_target_pairs={{3,1},{1,3},{6,4},{4,6}} | collective-permute-start | bytes 393224 | tf_op jit(solution)/shard_map/ppermute | solution.py:179
  956.1 2.8 copy-start.2
